TPU v7x, 128 devices: a whole 4x4x4 slice. The times are simulated.
128 devices in a mesh: row: 16 (over x, y_lo, core), col: 8 (over y_hi, z).
Axes of the slice: x: 4, y: 4 (y_hi: 2, y_lo: 2; y = y_hi * 2 + y_lo), z: 4, core: 2. Of those that a mesh axis runs over, the one named last changes fastest.
Arguments:
- pair_in: bfloat16 [768, 768, 128], P('row', 'col'), may hold values from -6 to 6
- coords: float32 [3, 768], P(None, 'row'), may hold values from -36 to 36
- chain_ids: int32 [768], P('row'), may hold values from 0 to 3, never falling along the last dimension, each value on 1 to 384 neighbouring positions
- coord_mask: int32 [768], P('row'), may hold values 0 or 1
- gain_tri: float32 [128], replicated, may hold values from 0.1 to 1.9
- gain_sum: float32 [128], replicated, may hold values from 0.1 to 1.9
- gain_attn: float32 [128], replicated, may hold values from 0.1 to 1.9
- w_tri_in: bfloat16 [128, 640], replicated, may hold values from -0.5 to 0.5
- w_tri_out: bfloat16 [128, 128], replicated, may hold values from -0.5 to 0.5
- w_bins: float32 [36, 128], replicated, may hold values from -3 to 3
- same_chain: float32 [128], replicated, may hold values from -6 to 6
- w_query: bfloat16 [128, 128], replicated, may hold values from -8 to 8
- w_attn: bfloat16 [128, 384], replicated, may hold values from -0.5 to 0.5
- w_bias: bfloat16 [128, 4], replicated, may hold values from -0.5 to 0.5
- w_attn_out: bfloat16 [128, 128], replicated, may hold values from -0.5 to 0.5
Outputs:
- pair_out: bfloat16 [768, 768, 128], P('row', 'col')
Inputs may be any that keep to these rules, and one draw needn't show every extreme that they name: `chain_ids`: chain numbers never fall along the residues, and no chain holds more than half of them.
All inputs are finite; a program needn't handle non-finite values. No bound on the sum of `coord_mask` on one device may be relied on, other than what follows from the above.
Results may differ from a plain program's by a relative error of at most 0.02.
Values may be sent and summed in bfloat16 or wider, within the bound.
No kernel may reach another device: no remote copies, remote signals or barrier semaphores. Data moves between devices by JAX's collectives and lax.ppermute only.
A program may use at most 192 MiB of HBM per device.

v0:
```python
import functools
import math

import jax
import jax.numpy as jnp
from jax import lax
from jax.experimental import pallas as pl
from jax.experimental.pallas import tpu as pltpu
from jax.sharding import Mesh
from jax.sharding import PartitionSpec as P

BF = jnp.bfloat16
F32 = jnp.float32
LOG2E = 1.4426950408889634
NT = (((1,), (1,)), ((), ()))
LANES = 128


def layer_norm(values, gain):
    center = values - jnp.mean(values, axis=-1, keepdims=True)
    spread = jnp.mean(center * center, axis=-1, keepdims=True)
    return center * lax.rsqrt(spread + 1e-05) * gain


def dot(a, b):
    return jnp.dot(a, b, preferred_element_type=F32)


def dot_nt(a, b):
    return lax.dot_general(a, b, NT, preferred_element_type=F32)


def exchange(x, axes):
    return lax.all_to_all(x, axes, split_axis=0, concat_axis=0, tiled=True)


def sides_kernel(x_ref, gain_ref, w_ref, out_ref, norm_sc, sc):
    n_rows, n_cols, ch = x_ref.shape
    n_out = out_ref.shape[1]
    third = n_rows // 3
    cut = LANES - n_cols

    def norm(i, carry):
        for u in range(4):
            norm_sc[i * 4 + u] = layer_norm(x_ref[i * 4 + u].astype(F32), gain_ref[...]).astype(BF)
        return carry

    lax.fori_loop(0, n_rows // 4, norm, 0, unroll=2)

    def sides(x):
        pr = dot_nt(w_ref[...], x)
        left = jax.nn.sigmoid(pr[:ch]) * pr[ch : 2 * ch]
        right = jax.nn.sigmoid(pr[2 * ch : 3 * ch]) * pr[3 * ch :]
        return left, right

    def put(row, value):
        sc[pl.ds(row, ch, stride=n_out), :] = value

    def main(s, carry):
        x = jnp.concatenate(
            [
                norm_sc[s],
                norm_sc[third + s, :cut],
                norm_sc[2 * third + s],
                norm_sc[third + s, cut : 2 * cut],
            ],
            axis=0,
        )
        left, right = sides(x)
        put(s, left[:, :LANES])
        put(third + s, left[:, LANES:])
        put(2 * third + s, right[:, :LANES])
        put(3 * third + s, right[:, LANES:])
        return carry

    lax.fori_loop(0, third, main, 0, unroll=4)

    is_left = lax.broadcasted_iota(jnp.int32, (ch, LANES), 1) < LANES // 2

    def rest(s, carry):
        one = norm_sc[third + s, 2 * cut :]
        two = norm_sc[third + third // 2 + s, 2 * cut :]
        left, right = sides(jnp.concatenate([one, two, one, two], axis=0))
        put(4 * third + s, jnp.where(is_left, left, right))
        return carry

    lax.fori_loop(0, third // 2, rest, 0, unroll=4)

    def emit(c, carry):
        out_ref[c] = sc[pl.ds(pl.multiple_of(c * n_out, 8), n_out), :].astype(BF)
        return carry

    lax.fori_loop(0, ch, emit, 0, unroll=16)


def make_sides(pair, gain, w_t):
    n_rows, n_cols, ch = pair.shape
    n_out = 2 * n_rows * n_cols // LANES
    return pl.pallas_call(
        sides_kernel,
        out_shape=jax.ShapeDtypeStruct((ch, n_out, LANES), BF),
        scratch_shapes=[
            pltpu.VMEM(pair.shape, BF),
            pltpu.VMEM((ch * n_out, LANES), F32),
        ],
        name="sides",
    )(pair, gain.reshape(1, ch), w_t)


def triangle_kernel(n_rh, n_core, n_col, n_rows, n_cols, in_ref, out_ref, l_sc, r_sc, p_sc):
    third = n_rows // 3
    cut = LANES - n_cols
    total = n_rh * n_core * n_rows
    n_pa = n_core * n_rows // n_col
    n_lt = total // n_core // LANES
    lane = lax.broadcasted_iota(jnp.int32, (third, LANES), 1)

    def middle(a, b, c):
        return jnp.where(
            lane < cut,
            pltpu.roll(a, cut, 1),
            jnp.where(lane < 2 * cut, pltpu.roll(b, 2 * cut, 1), jnp.where(lane < n_cols, c, 0.0)),
        )

    def unpack(rh, carry):
        for p in range(n_core):
            for c in range(n_col):
                blk = in_ref[(rh * n_core + p) * n_col + c].astype(F32)
                b = [blk[third * t : third * (t + 1)] for t in range(4)]
                last = blk[4 * third :]
                keep = [jnp.where(lane < n_cols, t, 0.0) for t in b]
                lc = jnp.concatenate([pltpu.roll(last, 2 * cut, 1), pltpu.roll(last, cut, 1)], axis=0)
                rc = jnp.concatenate([last, pltpu.roll(last, 3 * cut, 1)], axis=0)
                left = jnp.concatenate([keep[0], middle(b[0], b[1], lc), keep[1]], axis=0)
                right = jnp.concatenate([keep[2], middle(b[2], b[3], rc), keep[3]], axis=0)
                lanes = slice(c * LANES, (c + 1) * LANES)
                at_l = pl.multiple_of((rh * n_core + p) * n_rows, 16)
                at_r = pl.multiple_of((p * n_rh + rh) * n_rows, 16)
                l_sc[pl.ds(at_l, n_rows), lanes] = left.astype(BF)
                r_sc[pl.ds(at_r, n_rows), lanes] = right.astype(BF)
        return carry

    lax.fori_loop(0, n_rh, unpack, 0)
    wide = 2 * LANES
    for t in range(total // wide):
        part = dot_nt(l_sc[...], r_sc[t * wide : (t + 1) * wide, :])
        p_sc[2 * t] = part[:, :LANES]
        p_sc[2 * t + 1] = part[:, LANES:]

    def pack(rh, carry):
        for core in range(n_core):
            for c in range(n_col):
                rows = pl.ds(rh * n_core * n_rows + c, n_pa, stride=n_col)
                parts = [p_sc[core * n_lt + t, rows, :] for t in range(n_lt)]
                out_ref[(rh * n_core + core) * n_col + c] = jnp.concatenate(parts, axis=0).astype(BF)
        return carry

    lax.fori_loop(0, n_rh, pack, 0)


def triangle(sides, n_rh, n_core, n_col, n_rows, n_cols):
    total = n_rh * n_core * n_rows
    n_pa = n_core * n_rows // n_col
    n_lt = total // n_core // LANES
    return pl.pallas_call(
        functools.partial(triangle_kernel, n_rh, n_core, n_col, n_rows, n_cols),
        out_shape=jax.ShapeDtypeStruct((sides.shape[0], n_lt * n_pa, LANES), BF),
        scratch_shapes=[
            pltpu.VMEM((total, n_col * LANES), BF),
            pltpu.VMEM((total, n_col * LANES), BF),
            pltpu.VMEM((total // LANES, total, LANES), F32),
        ],
        name="triangle",
    )(sides)


def unit_norm(x, ones):
    center = x.astype(F32) - dot(x, ones[: x.shape[1]])
    square = center * center
    high = square.astype(BF)
    low = (square - high.astype(F32)).astype(BF)
    spread = dot(jnp.concatenate([high, low], axis=1), ones)
    return center * lax.rsqrt(spread + 1e-05)


def update_kernel(
    n_bins,
    back_ref,
    pair_ref,
    near_ref,
    far_ref,
    gain_tri_ref,
    gain_sum_ref,
    gain_attn_ref,
    wgo_ref,
    wout_ref,
    wbins_ref,
    wbias_ref,
    two_ref,
    normed_ref,
    bias_ref,
    sc,
):
    ch, n_in, _ = back_ref.shape
    n_q = far_ref.shape[1]
    n_lt = n_q // LANES
    n_pa = n_in // n_lt
    n_in8 = sc.shape[0] // ch
    n_heads = bias_ref.shape[1]
    tn = (((0,), (0,)), ((), ()))

    @pl.when(pl.program_id(0) == 0)
    def _():
        def widen(c, carry):
            sc[pl.ds(pl.multiple_of(c * n_in8, 8), n_in), :] = back_ref[c].astype(F32)
            return carry

        lax.fori_loop(0, ch, widen, 0, unroll=16)

    ones = jnp.full((2 * ch, ch), 1.0 / ch, BF)
    n_row = two_ref.shape[0]
    n_feat = wbins_ref.shape[0] // 3
    bin_at = lax.broadcasted_iota(jnp.int32, (n_feat, 1), 0)
    centres = 2.0 + 20.0 * bin_at.astype(F32) / (n_bins - 1)
    parts = []
    pairs = []
    feats = []
    for v in range(n_row):
        pa = pl.program_id(0) * n_row + v
        for t in range(n_lt):
            x = sc[pl.ds(t * n_pa + pa, ch, stride=n_in8), :]
            center = x - jnp.mean(x, axis=0, keepdims=True)
            spread = jnp.mean(center * center, axis=0, keepdims=True)
            parts.append((center * lax.rsqrt(spread + 1e-05) * gain_sum_ref[...]).astype(BF))
        pairs.append(pair_ref[0, :, v].reshape(n_q, ch))
        square = jnp.zeros((1, n_q), F32)
        for f in range(3):
            off = far_ref[f : f + 1, :] - near_ref[f, pa]
            square = square + off * off
        shared = (far_ref[3:4, :] == near_ref[3, pa]).astype(F32)
        mask = far_ref[4:5, :] * near_ref[4, pa]
        z = (jnp.sqrt(square + 1.0) - centres) * ((n_bins - 1) / 25.0)
        bins = jnp.exp(-(z * z)) * mask
        feats.append(jnp.where(bin_at < n_bins, bins, jnp.where(bin_at == n_bins, shared, 0.0)))
    tri = lax.dot_general(
        jnp.concatenate(parts, axis=1), wout_ref[...], tn, preferred_element_type=F32
    )
    pair = jnp.concatenate(pairs, axis=0)
    normed_pair = (unit_norm(pair, ones) * gain_tri_ref[...]).astype(BF)
    gate = jax.nn.sigmoid(dot(normed_pair, wgo_ref[...]))
    feats = jnp.concatenate(feats, axis=1)
    high = feats.astype(BF)
    low = (feats - high.astype(F32)).astype(BF)
    binned = lax.dot_general(
        jnp.concatenate([high, low, high], axis=0), wbins_ref[...], tn, preferred_element_type=F32
    )
    two = (pair.astype(F32) + gate * tri + binned).astype(BF)
    normed = (unit_norm(two, ones) * gain_attn_ref[...]).astype(BF)
    bias = dot_nt(wbias_ref[...], normed)[:n_heads].astype(BF)
    for v in range(n_row):
        two_ref[v] = two[v * n_q : (v + 1) * n_q]
        normed_ref[v] = normed[v * n_q : (v + 1) * n_q]
        bias_ref[v] = bias[:, v * n_q : (v + 1) * n_q]


def bin_weights(w_bins, same_chain):
    n_feat = -(-(w_bins.shape[0] + 1) // 16) * 16
    rows = jnp.concatenate([w_bins, same_chain[None]], axis=0)
    rows = jnp.pad(rows, ((0, n_feat - rows.shape[0]), (0, 0)))
    high = lax.reduce_precision(rows, 8, 7)
    return jnp.concatenate([high, high, rows - high], axis=0).astype(BF)


def update(back, moved, near, far, gains, wgo, wout, wbins, wbias_t, n_heads, n_bins, n_row=6):
    ch, n_in, _ = back.shape
    n_core, n_col, sub, half, _ = moved.shape
    n_q = n_col * half
    n_pa = n_core * sub
    n_in8 = -(-n_in // 8) * 8
    per = sub // n_row
    fixed = lambda i: (0, 0)
    row = lambda i: (i, 0, 0)
    return pl.pallas_call(
        functools.partial(update_kernel, n_bins),
        grid=(n_pa // n_row,),
        in_specs=[
            pl.BlockSpec(back.shape, lambda i: (0, 0, 0)),
            pl.BlockSpec((1, n_col, n_row, half, ch), lambda i: (i // per, 0, i % per, 0, 0)),
            pl.BlockSpec(memory_space=pltpu.SMEM),
            pl.BlockSpec(far.shape, fixed),
            pl.BlockSpec((1, ch), fixed),
            pl.BlockSpec((ch, 1), fixed),
            pl.BlockSpec((1, ch), fixed),
            pl.BlockSpec(wgo.shape, fixed),
            pl.BlockSpec(wout.shape, fixed),
            pl.BlockSpec(wbins.shape, fixed),
            pl.BlockSpec(wbias_t.shape, fixed),
        ],
        out_specs=[
            pl.BlockSpec((n_row, n_q, ch), row),
            pl.BlockSpec((n_row, n_q, ch), row),
            pl.BlockSpec((n_row, n_heads, n_q), row),
        ],
        out_shape=[
            jax.ShapeDtypeStruct((n_pa, n_q, ch), BF),
            jax.ShapeDtypeStruct((n_pa, n_q, ch), BF),
            jax.ShapeDtypeStruct((n_pa, n_heads, n_q), BF),
        ],
        scratch_shapes=[pltpu.VMEM((ch * n_in8, LANES), F32)],
        name="update",
    )(back, moved, near, far, gains[0], gains[1], gains[2], wgo, wout, wbins, wbias_t)


def project_kernel(
    core_ref, own_ref, other_ref, wq_ref, wk_ref, wv_ref, wg_ref, q_ref, k_ref, vt_ref, gate_ref
):
    n_heads, tall, n_k = vt_ref.shape[1:]
    head = wv_ref.shape[0] // n_heads
    first = core_ref[0] == 0
    n_row, n_q, ch = own_ref.shape
    own, other = own_ref[...], other_ref[...]
    full = jnp.concatenate(
        [jnp.where(first, own, other), jnp.where(first, other, own)], axis=1
    ).reshape(n_row * n_k, ch)
    own = own.reshape(n_row * n_q, ch)
    scale = LOG2E / math.sqrt(head)
    q_ref[...] = (dot(own, wq_ref[...]) * scale).astype(BF).reshape(n_row, n_q, ch)
    gate = jax.nn.sigmoid(dot_nt(wg_ref[...], own))
    k_ref[...] = dot(full, wk_ref[...]).astype(BF).reshape(n_row, n_k, ch)
    v_t = dot_nt(wv_ref[...], full).astype(BF)
    for r in range(n_row):
        gate_ref[r] = gate[:, r * n_q : (r + 1) * n_q]
        for h in range(n_heads):
            vt_ref[r, h, :head] = v_t[h * head : (h + 1) * head, r * n_k : (r + 1) * n_k]
            vt_ref[r, h, head:] = jnp.ones((tall - head, n_k), BF)


def project(core, own, other, wq, wk, wv_t, wg_t, n_heads, n_row=4):
    n_rows, n_q, ch = own.shape
    tall = ch // n_heads + 16
    row = lambda i: (i, 0, 0)
    fixed = pl.BlockSpec((ch, ch), lambda i: (0, 0))
    return pl.pallas_call(
        project_kernel,
        grid=(n_rows // n_row,),
        in_specs=[
            pl.BlockSpec(memory_space=pltpu.SMEM),
            pl.BlockSpec((n_row, n_q, ch), row),
            pl.BlockSpec((n_row, n_q, ch), row),
            fixed,
            fixed,
            fixed,
            fixed,
        ],
        out_specs=[
            pl.BlockSpec((n_row, n_q, ch), row),
            pl.BlockSpec((n_row, 2 * n_q, ch), row),
            pl.BlockSpec((n_row, n_heads, tall, 2 * n_q), lambda i: (i, 0, 0, 0)),
            pl.BlockSpec((n_row, ch, n_q), row),
        ],
        out_shape=[
            jax.ShapeDtypeStruct((n_rows, n_q, ch), BF),
            jax.ShapeDtypeStruct((n_rows, 2 * n_q, ch), BF),
            jax.ShapeDtypeStruct((n_rows, n_heads, tall, 2 * n_q), BF),
            jax.ShapeDtypeStruct((n_rows, ch, n_q), F32),
        ],
        name="project",
    )(core, own, other, wq, wk, wv_t, wg_t)


def attention_kernel(
    sub, q_ref, k_ref, vt_ref, gate_ref, two_ref, bias_ref, wo_ref, out_ref, raw_sc, bias_sc
):
    n_unit, n_k, _ = bias_sc.shape
    n_q, ch = q_ref.shape[1:]
    n_heads, tall, _ = vt_ref.shape[1:]
    head = ch // n_heads
    n_src, n_pay, _ = bias_ref.shape
    n_lt = n_q // LANES
    n_rh = n_src // 16
    n_col = n_q // sub // n_rh
    pairs = n_heads // 2

    @pl.when(pl.program_id(0) == 0)
    def _():
        def widen(d, carry):
            for v in range(4):
                at = pl.multiple_of((d * 4 + v) * n_pay, 8)
                for t in range(n_lt):
                    part = bias_ref[d * 4 + v, :, t * LANES : (t + 1) * LANES]
                    raw_sc[t, pl.ds(at, n_pay), :] = part.astype(F32) * -LOG2E
            return carry

        lax.fori_loop(0, n_src // 4, widen, 0)

        def turn(i, carry):
            s, h = i // n_heads, i % n_heads
            for u in range(n_lt):
                for t in range(n_lt):
                    rows = []
                    for r in range(16 * t, 16 * (t + 1)):
                        at = (r // sub * 2 + s) * n_col * n_pay + r % sub * n_heads + h
                        rows.append(raw_sc[u, pl.ds(at, n_col, stride=n_pay), :])
                    block = jnp.concatenate(rows, axis=0).T
                    at_k = pl.multiple_of(s * n_q + u * LANES, LANES)
                    at_q = pl.multiple_of(h % 2 * LANES, LANES)
                    bias_sc[t * pairs + h // 2, pl.ds(at_k, LANES), pl.ds(at_q, LANES)] = block
            return carry

        lax.fori_loop(0, 2 * n_heads, turn, 0)

    def row(r, carry):
        k = k_ref[r]
        lane_head = lax.broadcasted_iota(jnp.int32, (LANES, ch), 1) // head
        zero = jnp.zeros((), BF)

        def scores(n):
            t, hp = divmod(n, pairs)
            rows = q_ref[r, t * LANES : (t + 1) * LANES, :]
            both = [jnp.where(lane_head == 2 * hp + v, rows, zero) for v in range(2)]
            return dot_nt(k, jnp.concatenate(both, axis=0))

        s = scores(0)
        parts = []
        for n in range(n_unit):
            t, hp = divmod(n, pairs)
            ahead = scores(n + 1) if n + 1 < n_unit else None
            s = s - bias_sc[n]
            p = jnp.exp2(s - jnp.max(s, axis=0, keepdims=True)).astype(BF)
            both = vt_ref[r, 2 * hp : 2 * hp + 2].reshape(2 * tall, n_k)
            o = dot(both, p)
            for v in range(2):
                block = o[v * tall : (v + 1) * tall, v * LANES : (v + 1) * LANES]
                parts.append(block[:head] / block[head : head + 1])
            if hp == pairs - 1:
                cols = slice(t * LANES, (t + 1) * LANES)
                gated = (gate_ref[r, :, cols] * jnp.concatenate(parts, axis=0)).astype(BF)
                parts = []
                res = lax.dot_general(
                    gated, wo_ref[...], (((0,), (0,)), ((), ())), preferred_element_type=F32
                )
                out_ref[r, cols, :] = (two_ref[r, cols, :].astype(F32) + res).astype(BF)
            s = ahead
        return carry

    lax.fori_loop(0, q_ref.shape[0], row, 0, unroll=2)


def attention(q, k, vt, gate, two, bias, wo, sub, n_row=2):
    n_rows, n_q, ch = q.shape
    n_src, n_pay, _ = bias.shape
    n_heads = vt.shape[1]
    n_lt = n_q // LANES
    row = lambda i: (i, 0, 0)
    return pl.pallas_call(
        functools.partial(attention_kernel, sub),
        grid=(n_rows // n_row,),
        in_specs=[
            pl.BlockSpec((n_row, n_q, ch), row),
            pl.BlockSpec((n_row, 2 * n_q, ch), row),
            pl.BlockSpec((n_row,) + vt.shape[1:], lambda i: (i, 0, 0, 0)),
            pl.BlockSpec((n_row, ch, n_q), row),
            pl.BlockSpec((n_row, n_q, ch), row),
            pl.BlockSpec(bias.shape, lambda i: (0, 0, 0)),
            pl.BlockSpec(wo.shape, lambda i: (0, 0)),
        ],
        out_specs=pl.BlockSpec((n_row, n_q, ch), row),
        out_shape=jax.ShapeDtypeStruct(q.shape, BF),
        scratch_shapes=[
            pltpu.VMEM((n_lt, n_src * n_pay, LANES), F32),
            pltpu.VMEM((n_lt * n_heads // 2, 2 * n_q, 2 * LANES), F32),
        ],
        name="attention",
    )(q, k, vt, gate, two, bias, wo)


def body(
    pair_in,
    coords,
    chain_ids,
    coord_mask,
    gain_tri,
    gain_sum,
    gain_attn,
    w_tri_in,
    w_tri_out,
    w_bins,
    same_chain,
    w_query,
    w_attn,
    w_bias,
    w_attn_out,
):
    n_rh, n_core, n_col = (lax.axis_size(a) for a in ("rh", "core", "col"))
    rh, core, col = (lax.axis_index(a) for a in ("rh", "core", "col"))
    n_dev = n_rh * n_core * n_col
    every = ("rh", "core", "col")
    row_count, col_count, ch = pair_in.shape
    n_heads = w_bias.shape[1]
    n_bins = w_bins.shape[0]
    sub = row_count // n_col
    half = col_count // n_core
    n_pa = n_core * sub
    n_q = n_col * half

    to_move = (
        pair_in.reshape(sub, n_col, n_core, half, ch)
        .transpose(2, 1, 0, 3, 4)
        .reshape(n_core * n_col, sub, half, ch)
    )
    moved = exchange(to_move, ("core", "col"))
    moved = moved.reshape(n_core, n_col, sub, half, ch)

    packed = jnp.concatenate(
        [coords, chain_ids.astype(F32)[None], coord_mask.astype(F32)[None]], axis=0
    )
    packed = jnp.broadcast_to(packed, (n_rh * n_core, *packed.shape))
    known = exchange(packed, ("rh", "core"))
    known = known.reshape(n_rh, n_core, -1, row_count)
    near = lax.dynamic_index_in_dim(known, rh, 0, keepdims=False)
    near = near.transpose(1, 0, 2).reshape(-1, n_core, sub, n_col)
    near = lax.dynamic_index_in_dim(near, col, 3, keepdims=False).reshape(-1, n_pa)
    far = lax.dynamic_index_in_dim(known, core, 1, keepdims=False)
    far = far.transpose(1, 0, 2).reshape(-1, n_q)

    w_sides = w_tri_in[:, : 4 * ch].T
    sides = make_sides(pair_in, gain_tri, w_sides)
    sides = exchange(sides, every)
    product = triangle(sides, n_rh, n_core, n_col, row_count, col_count)
    back = exchange(product, every)
    two, normed, bias = update(
        back,
        moved,
        near,
        far,
        (gain_tri.reshape(1, ch), gain_sum.reshape(ch, 1), gain_attn.reshape(1, ch)),
        w_tri_in[:, 4 * ch :],
        w_tri_out,
        bin_weights(w_bins, same_chain),
        jnp.pad(w_bias.T, ((0, 16 - n_heads), (0, 0))),
        n_heads,
        n_bins,
    )

    n_pay = sub * n_heads
    spread = exchange(
        jnp.broadcast_to(
            bias.reshape(1, n_core, 1, n_pay, n_q), (n_rh, n_core, n_col, n_pay, n_q)
        ).reshape(n_dev, n_pay, n_q),
        every,
    )
    other = lax.ppermute(normed, every, [(d, d ^ n_col) for d in range(n_dev)])
    q, k, v_t, gate = project(
        core.reshape(1),
        normed,
        other,
        w_query,
        w_attn[:, :ch],
        w_attn[:, ch : 2 * ch].T,
        w_attn[:, 2 * ch :].T,
        n_heads,
    )
    result = attention(q, k, v_t, gate, two, spread, w_attn_out, sub)
    home = exchange(
        result.reshape(n_core, sub, n_col, half, ch)
        .transpose(0, 2, 1, 3, 4)
        .reshape(n_core * n_col, sub, half, ch),
        ("core", "col"),
    )
    return (
        home.reshape(n_core, n_col, sub, half, ch)
        .transpose(2, 1, 0, 3, 4)
        .reshape(row_count, col_count, ch)
    )


def solution(mesh):
    n_row, n_col = mesh.shape["row"], mesh.shape["col"]
    split = Mesh(mesh.devices.reshape(n_row // 2, 2, n_col), ("rh", "core", "col"))
    row = ("rh", "core")

    return jax.shard_map(
        body,
        mesh=split,
        in_specs=(P(row, "col", None), P(None, row), P(row), P(row)) + (P(),) * 11,
        out_specs=P(row, "col", None),
        check_vma=False,
    )
```

profile of v0, /device:TPU:1, one launch (start us, length us, event | category | flops | bytes accessed | tf_op | source)
XLA Modules:
  0.0 221.6 jit_solution(17787945313922520401)
XLA Ops:
  0.0 0.7 convert_bitcast_fusion
  0.7 0.7 pad_maximum_fusion.1
  1.4 0.7 reshape.69
  2.1 6.8 %all-to-all-start.3 = ((f32[16,1,240]{2,1,0:T(1,128)}), f32[16,1,240]{2,1,0:T(1,128)S(1)}, u32[]{:S(2)}, u32[]{:S(2)}) async-start(f32[16,1,240]{2,1,0:T(1,128)} %reshape.69), calls=%async_computation.3 | async-start | bytes 32768 | tf_op jit(solution)/shard_map/all_to_all | solution.py:34
  8.9 0.9 slice.15
  9.8 0.8 copy.42
  10.6 7.9 %sides.1 = bf16[128,72,128]{2,1,0:T(8,128)(2,1)} custom-call(bf16[48,96,128]{2,1,0:T(8,128)(2,1)} %x_ref.1, f32[1,128]{1,0:T(1,128)} %bitcast.48, bf16[512,128]{1,0:T(8,128)(2,1)} %bitcast.42), custom_call_target="tpu_custom_call" | custom-call | tf_op jit(solution)/shard_map/sides/pallas_call | solution.py:99
  18.4 0.0 copy-start.4
  18.4 0.0 all-to-all-done.3
  18.4 10.2 %all-to-all-start = ((bf16[128,72,128]{2,1,0:T(8,128)(2,1)}), bf16[128,72,128]{2,1,0:T(8,128)(2,1)S(1)}, u32[]{:S(2)}, u32[]{:S(2)}) async-start(bf16[128,72,128]{2,1,0:T(8,128)(2,1)} %sides.1), calls=%async_computation | async-start | bytes 4718592 | tf_op jit(solution)/shard_map/all_to_all | solution.py:34
  28.7 0.0 copy-done.4
  28.7 1.1 copy.35
  29.8 31.5 %all-to-all-done.in_ref = bf16[128,72,128]{2,1,0:T(8,128)(2,1)S(1)} async-done(((bf16[128,72,128]{2,1,0:T(8,128)(2,1)}), bf16[128,72,128]{2,1,0:T(8,128)(2,1)S(1)}, u32[]{:S(2)}, u32[]{:S(2)}) %all-to-all-start) | async-done | bytes 2359328 | tf_op jit(solution)/shard_map/all_to_all | solution.py:34
  61.3 0.0 copy-start.1
  61.3 1.4 copy-done.1
  62.7 5.2 %all-to-all-start.2 = ((bf16[16,6,48,128]{3,2,1,0:T(8,128)(2,1)}), bf16[16,6,48,128]{3,2,1,0:T(8,128)(2,1)S(1)}, u32[]{:S(2)}, u32[]{:S(2)}) async-start(bf16[16,6,48,128]{3,2,1,0:T(8,128)(2,1)} %bitcast.38), calls=%async_computation.2 | async-start | bytes 2359296 | tf_op jit(solution)/shard_map/all_to_all | solution.py:34
  67.9 6.0 %triangle.1 = bf16[128,36,128]{2,1,0:T(8,128)(2,1)} custom-call(bf16[128,72,128]{2,1,0:T(8,128)(2,1)} %copy-done.1), custom_call_target="tpu_custom_call" | custom-call | tf_op jit(solution)/shard_map/triangle/pallas_call | solution.py:165
  73.9 0.0 copy-start.8
  73.9 0.0 copy-start.7
  73.9 0.0 copy-start.6
  73.9 0.0 copy-start.9
  73.9 13.1 %all-to-all-done.2 = bf16[16,6,48,128]{3,2,1,0:T(8,128)(2,1)S(1)} async-done(((bf16[16,6,48,128]{3,2,1,0:T(8,128)(2,1)}), bf16[16,6,48,128]{3,2,1,0:T(8,128)(2,1)S(1)}, u32[]{:S(2)}, u32[]{:S(2)}) %all-to-all-start.2) | async-done | bytes 1179680 | tf_op jit(solution)/shard_map/all_to_all | solution.py:34
  87.0 0.0 copy-start.3
  87.0 1.0 copy-done.3
  88.0 3.8 %all-to-all-start.1 = ((bf16[128,36,128]{2,1,0:T(8,128)(2,1)}), bf16[128,36,128]{2,1,0:T(8,128)(2,1)S(1)}, u32[]{:S(2)}, u32[]{:S(2)}) async-start(bf16[128,36,128]{2,1,0:T(8,128)(2,1)} %triangle.1), calls=%async_computation.1 | async-start | bytes 2621440 | tf_op jit(solution)/shard_map/all_to_all | solution.py:34
  91.8 1.4 slice.16.wgo_ref
  93.2 0.0 copy-done.8
  93.2 0.7 copy.37.gain_sum_ref
  93.9 0.0 copy-done.7
  93.9 0.6 pad.9.wbias_ref
  94.5 0.0 copy-done.6
  94.5 0.0 copy-done.9
  94.5 0.6 pad_maximum_fusion.wbins_ref
  95.2 0.6 broadcast.13
  95.7 0.7 reduce.2
  96.5 0.1 reshape.70
  96.6 0.1 reshape.58
  96.7 0.2 dynamic-slice_reduce_fusion
  96.8 0.7 reshape.59.near_ref
  97.5 0.7 reshape.60.far_ref
  98.2 15.1 %all-to-all-done.1.back_ref = bf16[128,36,128]{2,1,0:T(8,128)(2,1)S(1)} async-done(((bf16[128,36,128]{2,1,0:T(8,128)(2,1)}), bf16[128,36,128]{2,1,0:T(8,128)(2,1)S(1)}, u32[]{:S(2)}, u32[]{:S(2)}) %all-to-all-start.1) | async-done | bytes 1179680 | tf_op jit(solution)/shard_map/all_to_all | solution.py:34
  113.4 0.0 copy-start.2
  113.4 1.1 copy-done.2
  114.4 8.3 %update.1 = (bf16[12,384,128]{2,1,0:T(8,128)(2,1)}, bf16[12,384,128]{2,1,0:T(8,128)(2,1)}, bf16[12,4,384]{2,1,0:T(4,128)(2,1)}) custom-call(bf16[128,36,128]{2,1,0:T(8,128)(2,1)} %copy-done.2, bf16[2,8,6,48,128]{4,3,2,1,0:T(8,128)(2,1)} %bitcast.37, f32[5,12]{1,0:T(8,128)} %reshape.59.near_ref, f32[5,384]{1,0:T(8,128)} %reshape.60.far_ref, ...), custom_call_target="tpu_custom_call" | custom-call | tf_op jit(solution)/shard_map/update/pallas_call | solution.py:283
  122.7 0.8 broadcast_in_dim.23
  123.5 1.7 broadcast_in_dim.24
  125.3 0.0 copy-start.5
  125.3 5.1 %all-to-all-start.4 = ((bf16[128,24,384]{2,1,0:T(8,128)(2,1)}), bf16[128,24,384]{2,1,0:T(8,128)(2,1)S(1)}, u32[]{:S(2)}, u32[]{:S(2)}) async-start(bf16[128,24,384]{2,1,0:T(8,128)(2,1)} %bitcast.35), calls=%async_computation.4 | async-start | bytes 4718592 | tf_op jit(solution)/shard_map/all_to_all | solution.py:34
  130.3 0.0 copy-done.5
  130.4 1.5 collective-permute-start
  131.8 1.4 fusion.1
  133.2 1.5 copy.43
  134.7 1.5 copy.44
  136.2 0.0 collective-permute-done.other_ref
  136.2 5.6 %project.1 = (bf16[12,384,128]{2,1,0:T(8,128)(2,1)}, bf16[12,768,128]{2,1,0:T(8,128)(2,1)}, bf16[12,4,48,768]{3,2,1,0:T(8,128)(2,1)}, f32[12,128,384]{2,1,0:T(8,128)}) custom-call(s32[1]{0:T(128)} %bitcast.core_ref, bf16[12,384,128]{2,1,0:T(8,128)(2,1)} %get-tuple-element.12.own_ref, bf16[12,384,128]{2,1,0:T(8,128)(2,1)} %collective-permute-done.other_ref, ...), custom_call_target="tpu_custom_call" | custom-call | tf_op jit(solution)/shard_map/project/pallas_call | solution.py:343
  141.8 21.3 %all-to-all-done.4.bias_ref = bf16[128,24,384]{2,1,0:T(8,128)(2,1)S(1)} async-done(((bf16[128,24,384]{2,1,0:T(8,128)(2,1)}), bf16[128,24,384]{2,1,0:T(8,128)(2,1)S(1)}, u32[]{:S(2)}, u32[]{:S(2)}) %all-to-all-start.4) | async-done | bytes 2359328 | tf_op jit(solution)/shard_map/all_to_all | solution.py:34
  163.1 0.0 copy-start
  163.1 1.4 copy-done
  164.5 31.4 %attention.1 = bf16[12,384,128]{2,1,0:T(8,128)(2,1)} custom-call(bf16[12,384,128]{2,1,0:T(8,128)(2,1)} %get-tuple-element.13.q_ref, bf16[12,768,128]{2,1,0:T(8,128)(2,1)} %get-tuple-element.14.k_ref, bf16[12,4,48,768]{3,2,1,0:T(8,128)(2,1)} %get-tuple-element.15.vt_ref, f32[12,128,384]{2,1,0:T(8,128)} %get-tuple-element.16.gate_ref, ...), custom_call_target="tpu_custom_call" | custom-call | tf_op jit(solution)/shard_map/attention/pallas_call | solution.py:455
  195.9 1.3 copy.40
  197.2 23.2 %all_to_all.30 = bf16[16,6,48,128]{3,2,1,0:T(8,128)(2,1)S(1)} all-to-all(bf16[16,6,48,128]{3,2,1,0:T(8,128)(2,1)S(1)} %bitcast.39), channel_id=1, replica_groups=mesh['rh'=8,'core'=2,'col'=8] {'core','col'}, dimensions={0} | all-to-all | bytes 2359296 | tf_op jit(solution)/shard_map/all_to_all | solution.py:34
  220.4 1.1 copy.41
  (5 shorter events, 0.1 us)
Async XLA Ops:
  2.1 16.4 %all-to-all-start.3 = ((f32[16,1,240]{2,1,0:T(1,128)}), f32[16,1,240]{2,1,0:T(1,128)S(1)}, u32[]{:S(2)}, u32[]{:S(2)}) async-start(f32[16,1,240]{2,1,0:T(1,128)} %reshape.69), calls=%async_computation.3 | async-start | bytes 32768 | tf_op jit(solution)/shard_map/all_to_all | solution.py:34
  18.4 10.2 %copy-start.4 = (bf16[48,96,128]{2,1,0:T(8,128)(2,1)S(1)}, bf16[48,96,128]{2,1,0:T(8,128)(2,1)}, u32[]{:S(2)}) copy-start(bf16[48,96,128]{2,1,0:T(8,128)(2,1)} %x_ref.1) | copy-start | bytes 3538948
  18.4 42.8 %all-to-all-start = ((bf16[128,72,128]{2,1,0:T(8,128)(2,1)}), bf16[128,72,128]{2,1,0:T(8,128)(2,1)S(1)}, u32[]{:S(2)}, u32[]{:S(2)}) async-start(bf16[128,72,128]{2,1,0:T(8,128)(2,1)} %sides.1), calls=%async_computation | async-start | bytes 4718592 | tf_op jit(solution)/shard_map/all_to_all | solution.py:34
  61.3 1.4 copy-start.1
  62.7 24.3 %all-to-all-start.2 = ((bf16[16,6,48,128]{3,2,1,0:T(8,128)(2,1)}), bf16[16,6,48,128]{3,2,1,0:T(8,128)(2,1)S(1)}, u32[]{:S(2)}, u32[]{:S(2)}) async-start(bf16[16,6,48,128]{3,2,1,0:T(8,128)(2,1)} %bitcast.38), calls=%async_computation.2 | async-start | bytes 2359296 | tf_op jit(solution)/shard_map/all_to_all | solution.py:34
  73.9 19.3 %copy-start.8 = (f32[128]{0:T(128)S(1)}, f32[128]{0:T(128)}, u32[]{:S(2)}) copy-start(f32[128]{0:T(128)} %param.20) | copy-start | bytes 1540
  73.9 20.0 %copy-start.7 = (bf16[128,4]{0,1:T(4,128)(2,1)S(1)}, bf16[128,4]{0,1:T(4,128)(2,1)}, u32[]{:S(2)}) copy-start(bf16[128,4]{0,1:T(4,128)(2,1)} %param.28) | copy-start | bytes 3076
  73.9 20.6 %copy-start.6 = (f32[36,128]{1,0:T(8,128)S(1)}, f32[36,128]{1,0:T(8,128)}, u32[]{:S(2)}) copy-start(f32[36,128]{1,0:T(8,128)} %param.24) | copy-start | bytes 55300
  73.9 20.6 %copy-start.9 = (f32[128]{0:T(128)S(1)}, f32[128]{0:T(128)}, u32[]{:S(2)}) copy-start(f32[128]{0:T(128)} %param.25) | copy-start | bytes 1540
  87.0 1.0 copy-start.3
  88.0 25.4 %all-to-all-start.1 = ((bf16[128,36,128]{2,1,0:T(8,128)(2,1)}), bf16[128,36,128]{2,1,0:T(8,128)(2,1)S(1)}, u32[]{:S(2)}, u32[]{:S(2)}) async-start(bf16[128,36,128]{2,1,0:T(8,128)(2,1)} %triangle.1), calls=%async_computation.1 | async-start | bytes 2621440 | tf_op jit(solution)/shard_map/all_to_all | solution.py:34
  113.4 1.1 copy-start.2
  125.3 5.1 %copy-start.5 = (bf16[12,384,128]{2,1,0:T(8,128)(2,1)S(1)}, bf16[12,384,128]{2,1,0:T(8,128)(2,1)}, u32[]{:S(2)}) copy-start(bf16[12,384,128]{2,1,0:T(8,128)(2,1)} %get-tuple-element.12.own_ref) | copy-start | bytes 3538948
  125.3 37.8 %all-to-all-start.4 = ((bf16[128,24,384]{2,1,0:T(8,128)(2,1)}), bf16[128,24,384]{2,1,0:T(8,128)(2,1)S(1)}, u32[]{:S(2)}, u32[]{:S(2)}) async-start(bf16[128,24,384]{2,1,0:T(8,128)(2,1)} %bitcast.35), calls=%async_computation.4 | async-start | bytes 4718592 | tf_op jit(solution)/shard_map/all_to_all | solution.py:34
  130.4 5.8 %collective-permute-start = (bf16[12,384,128]{2,1,0:T(8,128)(2,1)S(1)}, bf16[12,384,128]{2,1,0:T(8,128)(2,1)}, u32[]{:S(2)}, u32[]{:S(2)}) collective-permute-start(bf16[12,384,128]{2,1,0:T(8,128)(2,1)S(1)} %copy-done.5), channel_id=1, source_target_pairs={{0,8},{1,9},{2,10},{3,11},{4,12},{5,13},{6,14},{7,15},{8,0},{9,1},... | collective-permute-start | bytes 3538952 | tf_op jit(solution)/shard_map/ppermute | solution.py:552
  163.1 1.4 copy-start
where the time goes:
time: 223 us; the launch traced here: 222 us
  waiting for transfers between devices  81 us (36%)
  Pallas kernels  59.2 us (27%)
  starting transfers between devices  32.6 us (15%)
  blocking collectives  23.2 us (10%)
  local copies, waits for them, and re-layouts  22.8 us (10%)
  other arithmetic  2.72 us (1%)
    all_to_all x5, waiting for transfers between devices, exchange(): return lax.all_to_all(x, axes, split_axis=0, concat_axis=0, tiled=True)  81 us
    pallas_call x1, Pallas kernels, attention(): pl.pallas_call(functools.partial(attention_kernel, sub), grid=(n_rows //...  31.4 us
    all_to_all x5, starting transfers between devices, exchange(): return lax.all_to_all(x, axes, split_axis=0, concat_axis=0, tiled=True)  31.1 us
    all_to_all x1, blocking collectives, exchange(): return lax.all_to_all(x, axes, split_axis=0, concat_axis=0, tiled=True)  23.2 us
    unnamed x25, local copies, waits for them, and re-layouts  9.41 us
    pallas_call x1, Pallas kernels, update(): pl.pallas_call(functools.partial(update_kernel, n_bins), grid=(n_pa // n_...  8.3 us
    pallas_call x1, Pallas kernels, make_sides(): pl.pallas_call(sides_kernel, out_shape=jax.ShapeDtypeStruct((ch, n_out, L...  7.88 us
    pallas_call x1, Pallas kernels, triangle(): pl.pallas_call(functools.partial(triangle_kernel, n_rh, n_core, n_col, n_...  6 us
  transfers between devices with their start and end apart: 6, of which 4 were waited for; matrix products, arithmetic and copies ran while one was open for 6% of the time, Pallas kernels for 9%

commit v1 on v0

--- a/solution.py
+++ b/solution.py
@@ -34,8 +34,13 @@
     return lax.all_to_all(x, axes, split_axis=0, concat_axis=0, tiled=True)
 
 
-def sides_kernel(x_ref, gain_ref, w_ref, out_ref, norm_sc, sc):
+def sides_kernel(col_ref, x_ref, gain_ref, w_ref, out_ref, *rest_refs):
+    piece_refs, norm_sc, sc = rest_refs[:-2], rest_refs[-2], rest_refs[-1]
     n_rows, n_cols, ch = x_ref.shape
+    n_col = len(piece_refs)
+    for shift, piece_ref in enumerate(piece_refs):
+        for a in range(n_rows // n_col):
+            piece_ref[a] = x_ref[a * n_col + (col_ref[0] + shift) % n_col]
     n_out = out_ref.shape[1]
     third = n_rows // 3
     cut = LANES - n_cols
@@ -93,18 +98,20 @@
     lax.fori_loop(0, ch, emit, 0, unroll=16)
 
 
-def make_sides(pair, gain, w_t):
+def make_sides(col, pair, gain, w_t, n_col):
     n_rows, n_cols, ch = pair.shape
     n_out = 2 * n_rows * n_cols // LANES
+    piece = jax.ShapeDtypeStruct((n_rows // n_col, n_cols, ch), BF)
     return pl.pallas_call(
         sides_kernel,
-        out_shape=jax.ShapeDtypeStruct((ch, n_out, LANES), BF),
+        in_specs=[pl.BlockSpec(memory_space=pltpu.SMEM)] + [pl.BlockSpec()] * 3,
+        out_shape=[jax.ShapeDtypeStruct((ch, n_out, LANES), BF)] + [piece] * n_col,
         scratch_shapes=[
             pltpu.VMEM(pair.shape, BF),
             pltpu.VMEM((ch * n_out, LANES), F32),
         ],
         name="sides",
-    )(pair, gain.reshape(1, ch), w_t)
+    )(col, pair, gain.reshape(1, ch), w_t)
 
 
 def triangle_kernel(n_rh, n_core, n_col, n_rows, n_cols, in_ref, out_ref, l_sc, r_sc, p_sc):
@@ -185,8 +192,10 @@
 
 def update_kernel(
     n_bins,
+    place_ref,
     back_ref,
-    pair_ref,
+    keep_ref,
+    other_ref,
     near_ref,
     far_ref,
     gain_tri_ref,
@@ -206,6 +215,7 @@
     n_lt = n_q // LANES
     n_pa = n_in // n_lt
     n_in8 = sc.shape[0] // ch
+    n_col = keep_ref.shape[0]
     n_heads = bias_ref.shape[1]
     tn = (((0,), (0,)), ((), ()))
 
@@ -232,7 +242,10 @@
             center = x - jnp.mean(x, axis=0, keepdims=True)
             spread = jnp.mean(center * center, axis=0, keepdims=True)
             parts.append((center * lax.rsqrt(spread + 1e-05) * gain_sum_ref[...]).astype(BF))
-        pairs.append(pair_ref[0, :, v].reshape(n_q, ch))
+        mine = place_ref[0] == pl.program_id(0) * n_row // (n_pa // 2)
+        for c in range(n_col):
+            shift = (place_ref[1] + n_col - c) % n_col
+            pairs.append(jnp.where(mine, keep_ref[shift, v], other_ref[shift, v]))
         square = jnp.zeros((1, n_q), F32)
         for f in range(3):
             off = far_ref[f : f + 1, :] - near_ref[f, pa]
@@ -271,11 +284,11 @@
     return jnp.concatenate([high, high, rows - high], axis=0).astype(BF)
 
 
-def update(back, moved, near, far, gains, wgo, wout, wbins, wbias_t, n_heads, n_bins, n_row=6):
+def update(place, back, keep, other, near, far, gains, wgo, wout, wbins, wbias_t, n_heads, n_bins, n_row=6):
     ch, n_in, _ = back.shape
-    n_core, n_col, sub, half, _ = moved.shape
+    n_col, sub, half, _ = keep.shape
     n_q = n_col * half
-    n_pa = n_core * sub
+    n_pa = 2 * sub
     n_in8 = -(-n_in // 8) * 8
     per = sub // n_row
     fixed = lambda i: (0, 0)
@@ -284,8 +297,10 @@
         functools.partial(update_kernel, n_bins),
         grid=(n_pa // n_row,),
         in_specs=[
+            pl.BlockSpec(memory_space=pltpu.SMEM),
             pl.BlockSpec(back.shape, lambda i: (0, 0, 0)),
-            pl.BlockSpec((1, n_col, n_row, half, ch), lambda i: (i // per, 0, i % per, 0, 0)),
+            pl.BlockSpec((n_col, n_row, half, ch), lambda i: (0, i % per, 0, 0)),
+            pl.BlockSpec((n_col, n_row, half, ch), lambda i: (0, i % per, 0, 0)),
             pl.BlockSpec(memory_space=pltpu.SMEM),
             pl.BlockSpec(far.shape, fixed),
             pl.BlockSpec((1, ch), fixed),
@@ -308,7 +323,7 @@
         ],
         scratch_shapes=[pltpu.VMEM((ch * n_in8, LANES), F32)],
         name="update",
-    )(back, moved, near, far, gains[0], gains[1], gains[2], wgo, wout, wbins, wbias_t)
+    )(place, back, keep, other, near, far, gains[0], gains[1], gains[2], wgo, wout, wbins, wbias_t)
 
 
 def project_kernel(
@@ -503,34 +518,43 @@
     n_pa = n_core * sub
     n_q = n_col * half
 
-    to_move = (
-        pair_in.reshape(sub, n_col, n_core, half, ch)
-        .transpose(2, 1, 0, 3, 4)
-        .reshape(n_core * n_col, sub, half, ch)
-    )
-    moved = exchange(to_move, ("core", "col"))
-    moved = moved.reshape(n_core, n_col, sub, half, ch)
+    w_sides = w_tri_in[:, : 4 * ch].T
+    sides, *pieces = make_sides(col.reshape(1), pair_in, gain_tri, w_sides, n_col)
+    sides = exchange(sides, every)
+
+    pieces = [pieces[0]] + [
+        lax.ppermute(pieces[d], "col", [(i, (i + d) % n_col) for i in range(n_col)])
+        for d in range(1, n_col)
+    ]
+    whole = jnp.stack(pieces).reshape(n_col, sub, n_core, half, ch)
+    keep = lax.dynamic_index_in_dim(whole, core, 2, keepdims=False)
+    give = lax.dynamic_index_in_dim(whole, 1 - core, 2, keepdims=False)
+    other_pair = lax.ppermute(give, "core", [(0, 1), (1, 0)])
 
     packed = jnp.concatenate(
         [coords, chain_ids.astype(F32)[None], coord_mask.astype(F32)[None]], axis=0
-    )
-    packed = jnp.broadcast_to(packed, (n_rh * n_core, *packed.shape))
-    known = exchange(packed, ("rh", "core"))
-    known = known.reshape(n_rh, n_core, -1, row_count)
+    ).reshape(1, -1)
+    n_row = n_rh * n_core
+    step = 1
+    while step < n_row:
+        swap = [(r, r ^ step) for r in range(n_row)]
+        packed = jnp.concatenate([packed, lax.ppermute(packed, ("rh", "core"), swap)], axis=0)
+        step *= 2
+    at = jnp.arange(n_row) ^ (rh * n_core + core)
+    known = packed[at].reshape(n_rh, n_core, -1, row_count)
     near = lax.dynamic_index_in_dim(known, rh, 0, keepdims=False)
     near = near.transpose(1, 0, 2).reshape(-1, n_core, sub, n_col)
     near = lax.dynamic_index_in_dim(near, col, 3, keepdims=False).reshape(-1, n_pa)
     far = lax.dynamic_index_in_dim(known, core, 1, keepdims=False)
     far = far.transpose(1, 0, 2).reshape(-1, n_q)
 
-    w_sides = w_tri_in[:, : 4 * ch].T
-    sides = make_sides(pair_in, gain_tri, w_sides)
-    sides = exchange(sides, every)
     product = triangle(sides, n_rh, n_core, n_col, row_count, col_count)
     back = exchange(product, every)
     two, normed, bias = update(
+        jnp.stack([core, col]),
         back,
-        moved,
+        keep,
+        other_pair,
         near,
         far,
         (gain_tri.reshape(1, ch), gain_sum.reshape(ch, 1), gain_attn.reshape(1, ch)),

time: 223 us -> 218 us (0.978)
  waiting for transfers between devices: 81 us -> 50.4 us
  starting transfers between devices: 32.6 us -> 53 us
  local copies, waits for them, and re-layouts: 22.8 us -> 28.8 us
    all_to_all x5 -> x3, waiting for transfers between devices: 81 us -> 21.4 us  [exchange(): return lax.all_to_all(x, axes, split_axis=0, concat_axis=0, tiled=True)]
    ppermute x0 -> x12, waiting for transfers between devices: none -> 29 us  [the longest x7 20.2 us: body(): lax.ppermute(pieces[d], 'col', [(i, (i + d) % n_col) for i in range(n_col)])]
    ppermute x0 -> x12, starting transfers between devices: none -> 22.5 us  [the longest x7 16.5 us: body(): lax.ppermute(pieces[d], 'col', [(i, (i + d) % n_col) for i in range(n_col)])]
    unnamed x25 -> x36, local copies, waits for them, and re-layouts: 9.41 us -> 14.3 us
    all_to_all x5 -> x3, starting transfers between devices: 31.1 us -> 29.4 us  [exchange(): return lax.all_to_all(x, axes, split_axis=0, concat_axis=0, tiled=True)]
  transfers between devices with their start and end apart: 6 -> 16, of which waited for: 4 -> 3; matrix products, arithmetic and copies ran while one was open for 6% -> 9% of each run, Pallas kernels for 9% -> 5%
where the time goes in v1:
time: 218 us; the launch traced here: 217 us
  Pallas kernels  59.8 us (27%)
  starting transfers between devices  53 us (24%)
  waiting for transfers between devices  50.4 us (23%)
  local copies, waits for them, and re-layouts  28.8 us (13%)
  blocking collectives  23.2 us (11%)
    pallas_call x1, Pallas kernels, attention(): pl.pallas_call(functools.partial(attention_kernel, sub), grid=(n_rows //...  31.4 us
    all_to_all x3, starting transfers between devices, exchange(): return lax.all_to_all(x, axes, split_axis=0, concat_axis=0, tiled=True)  29.4 us
    all_to_all x1, blocking collectives, exchange(): return lax.all_to_all(x, axes, split_axis=0, concat_axis=0, tiled=True)  23.2 us
    all_to_all x3, waiting for transfers between devices, exchange(): return lax.all_to_all(x, axes, split_axis=0, concat_axis=0, tiled=True)  21.4 us
    ppermute x7, waiting for transfers between devices, body(): lax.ppermute(pieces[d], 'col', [(i, (i + d) % n_col) for i in range(n_col)])  20.2 us
    ppermute x7, starting transfers between devices, body(): lax.ppermute(pieces[d], 'col', [(i, (i + d) % n_col) for i in range(n_col)])  16.5 us
    unnamed x36, local copies, waits for them, and re-layouts  14.3 us
    ppermute x4, waiting for transfers between devices, body(): lax.ppermute(packed, ('rh', 'core'), swap)  8.72 us
  transfers between devices with their start and end apart: 16, of which 3 were waited for; matrix products, arithmetic and copies ran while one was open for 9% of the time, Pallas kernels for 5%

profile of v1, /device:TPU:1, one launch (start us, length us, event | category | flops | bytes accessed | tf_op | source)
XLA Modules:
  0.0 217.2 jit_solution(15262293937849238980)
XLA Ops:
  0.0 0.9 slice.15
  0.9 0.8 copy.59
  1.7 8.3 %sides.1 = (bf16[128,72,128]{2,1,0:T(8,128)(2,1)}, bf16[6,96,128]{2,1,0:T(8,128)(2,1)}, bf16[6,96,128]{2,1,0:T(8,128)(2,1)}, bf16[6,96,128]{2,1,0:T(8,128)(2,1)}...) custom-call(s32[1]{0:T(128)} %bitcast.1.col_ref, ...), custom_call_target="tpu_custom_call" | custom-call | tf_op jit(solution)/shard_map/sides/pallas_call | solution.py:105
  10.0 0.0 copy-start.5
  10.0 0.0 copy-start.8
  10.0 11.5 %all-to-all-start = ((bf16[128,72,128]{2,1,0:T(8,128)(2,1)}), bf16[128,72,128]{2,1,0:T(8,128)(2,1)S(1)}, u32[]{:S(2)}, u32[]{:S(2)}) async-start(bf16[128,72,128]{2,1,0:T(8,128)(2,1)} %get-tuple-element.21), calls=%async_computation | async-start | bytes 4718592 | tf_op jit(solution)/shard_map/all_to_all | solution.py:34
  21.5 1.6 collective-permute-start
  23.1 2.9 %collective-permute-start.1 = (bf16[6,96,128]{2,1,0:T(8,128)(2,1)}, bf16[6,96,128]{2,1,0:T(8,128)(2,1)}, u32[]{:S(2)}, u32[]{:S(2)}) collective-permute-start(bf16[6,96,128]{2,1,0:T(8,128)(2,1)} %get-tuple-element.24), channel_id=1, source_target_pairs={{0,2},{1,3},{2,4},{3,5},{4,6},{5,7},{6,0},{7,1},{8,10},{9,11},{10,... | collective-permute-start | bytes 442376 | tf_op jit(solution)/shard_map/ppermute | solution.py:526
  26.0 3.5 %collective-permute-start.2 = (bf16[6,96,128]{2,1,0:T(8,128)(2,1)}, bf16[6,96,128]{2,1,0:T(8,128)(2,1)}, u32[]{:S(2)}, u32[]{:S(2)}) collective-permute-start(bf16[6,96,128]{2,1,0:T(8,128)(2,1)} %get-tuple-element.25), channel_id=1, source_target_pairs={{0,3},{1,4},{2,5},{3,6},{4,7},{5,0},{6,1},{7,2},{8,11},{9,12},{10,... | collective-permute-start | bytes 442376 | tf_op jit(solution)/shard_map/ppermute | solution.py:526
  29.4 0.1 collective-permute-start.3
  29.6 0.1 reshape.82
  29.7 1.5 collective-permute-start.8
  31.3 0.6 pad_maximum_fusion.wbins_ref
  31.9 0.9 constant_dynamic-update-slice_fusion.7
  32.8 0.6 fusion.1
  33.4 3.1 %collective-permute-start.4 = (bf16[6,96,128]{2,1,0:T(8,128)(2,1)}, bf16[6,96,128]{2,1,0:T(8,128)(2,1)}, u32[]{:S(2)}, u32[]{:S(2)}) collective-permute-start(bf16[6,96,128]{2,1,0:T(8,128)(2,1)} %get-tuple-element.27), channel_id=1, source_target_pairs={{0,5},{1,6},{2,7},{3,0},{4,1},{5,2},{6,3},{7,4},{8,13},{9,14},{10,... | collective-permute-start | bytes 442376 | tf_op jit(solution)/shard_map/ppermute | solution.py:526
  36.5 20.2 %collective-permute-done = bf16[6,96,128]{2,1,0:T(8,128)(2,1)} collective-permute-done((bf16[6,96,128]{2,1,0:T(8,128)(2,1)}, bf16[6,96,128]{2,1,0:T(8,128)(2,1)}, u32[]{:S(2)}, u32[]{:S(2)}) %collective-permute-start) | collective-permute-done | bytes 147488 | tf_op jit(solution)/shard_map/ppermute | solution.py:526
  56.7 4.3 %collective-permute-start.5 = (bf16[6,96,128]{2,1,0:T(8,128)(2,1)}, bf16[6,96,128]{2,1,0:T(8,128)(2,1)}, u32[]{:S(2)}, u32[]{:S(2)}) collective-permute-start(bf16[6,96,128]{2,1,0:T(8,128)(2,1)} %get-tuple-element.28), channel_id=1, source_target_pairs={{0,6},{1,7},{2,0},{3,1},{4,2},{5,3},{6,4},{7,5},{8,14},{9,15},{10,... | collective-permute-start | bytes 442376 | tf_op jit(solution)/shard_map/ppermute | solution.py:526
  61.0 0.9 constant_dynamic-update-slice_fusion.6
  61.9 1.1 collective-permute-start.6
  63.0 0.9 constant_dynamic-update-slice_fusion.5
  64.0 0.1 collective-permute-start.9
  64.1 0.9 constant_dynamic-update-slice_fusion.4
  65.0 1.4 copy-done.1
  66.4 6.0 %triangle.1 = bf16[128,36,128]{2,1,0:T(8,128)(2,1)} custom-call(bf16[128,72,128]{2,1,0:T(8,128)(2,1)} %copy-done.1), custom_call_target="tpu_custom_call" | custom-call | tf_op jit(solution)/shard_map/triangle/pallas_call | solution.py:172
  72.4 8.5 %all-to-all-start.1 = ((bf16[128,36,128]{2,1,0:T(8,128)(2,1)}), bf16[128,36,128]{2,1,0:T(8,128)(2,1)S(1)}, u32[]{:S(2)}, u32[]{:S(2)}) async-start(bf16[128,36,128]{2,1,0:T(8,128)(2,1)} %triangle.1), calls=%async_computation.1 | async-start | bytes 2621440 | tf_op jit(solution)/shard_map/all_to_all | solution.py:34
  81.0 0.9 constant_dynamic-update-slice_fusion.3
  81.9 0.9 constant_dynamic-update-slice_fusion.2
  82.9 0.9 constant_dynamic-update-slice_fusion.1
  83.8 0.9 constant_dynamic-update-slice_fusion
  84.7 0.0 copy-start.9
  84.8 0.0 copy-start.7
  84.8 1.1 dynamic-slice_bitcast_fusion
  85.9 1.1 collective-permute-start.7
  87.0 0.8 collective-permute-start.10
  87.7 8.7 %collective-permute-done.10 = f32[4,240]{1,0:T(4,128)S(1)} collective-permute-done((f32[4,240]{1,0:T(4,128)S(1)}, f32[4,240]{1,0:T(4,128)S(1)}, u32[]{:S(2)}, u32[]{:S(2)}) %collective-permute-start.10) | collective-permute-done | bytes 3872 | tf_op jit(solution)/shard_map/ppermute | solution.py:541
  96.5 2.5 %collective-permute-start.11 = (f32[8,240]{1,0:T(8,128)S(1)}, f32[8,240]{1,0:T(8,128)S(1)}, u32[]{:S(2)}, u32[]{:S(2)}) collective-permute-start(f32[8,240]{1,0:T(8,128)S(1)} %pad_maximum_fusion.1), channel_id=1, source_target_pairs={{0,64},{8,72},{16,80},{24,88},{32,96},{40,104},{48,112},{56,120},{... | collective-permute-start | bytes 23048 | tf_op jit(solution)/shard_map/ppermute | solution.py:541
  98.9 0.6 pad_add_fusion.place_ref
  99.5 1.4 slice.16.wgo_ref
  100.9 0.7 copy.53.gain_sum_ref
  101.6 0.6 pad.9.wbias_ref
  102.3 0.6 gather_fusion
  102.8 0.1 reshape.83
  102.9 0.1 reshape.84
  103.0 0.2 dynamic-slice_reduce_fusion
  103.2 0.7 reshape.85.near_ref
  103.9 0.7 reshape.86.far_ref
  104.6 0.8 copy-done.4
  105.4 0.5 copy-done.2
  105.8 8.4 %update.1 = (bf16[12,384,128]{2,1,0:T(8,128)(2,1)}, bf16[12,384,128]{2,1,0:T(8,128)(2,1)}, bf16[12,4,384]{2,1,0:T(4,128)(2,1)}) custom-call(s32[2]{0:T(128)} %pad_add_fusion.place_ref, bf16[128,36,128]{2,1,0:T(8,128)(2,1)} %copy-done.2, bf16[8,6,48,128]{3,2,1,0:T(8,128)(2,1)} %get-tuple-element.38.keep_ref, bf16[8,6,48,128]{3,2,1,0:T(8,128)(2,1)} %copy-done.4, ...), custom_call_target="tpu_custom_call" | custom-call | tf_op jit(solution)/shard_map/update/pallas_call | solution.py:296
  114.3 0.8 broadcast_in_dim.20
  115.1 1.7 broadcast_in_dim.21
  116.8 9.4 %all-to-all-start.2 = ((bf16[128,24,384]{2,1,0:T(8,128)(2,1)}), bf16[128,24,384]{2,1,0:T(8,128)(2,1)S(1)}, u32[]{:S(2)}, u32[]{:S(2)}) async-start(bf16[128,24,384]{2,1,0:T(8,128)(2,1)} %bitcast.51), calls=%async_computation.2 | async-start | bytes 4718592 | tf_op jit(solution)/shard_map/all_to_all | solution.py:34
  126.2 1.1 collective-permute-start.12
  127.3 1.4 fusion.2
  128.8 1.5 copy.62
  130.2 1.5 copy.63
  131.7 5.7 %project.1 = (bf16[12,384,128]{2,1,0:T(8,128)(2,1)}, bf16[12,768,128]{2,1,0:T(8,128)(2,1)}, bf16[12,4,48,768]{3,2,1,0:T(8,128)(2,1)}, f32[12,128,384]{2,1,0:T(8,128)}) custom-call(s32[1]{0:T(128)} %bitcast.core_ref, bf16[12,384,128]{2,1,0:T(8,128)(2,1)} %get-tuple-element.30.own_ref, bf16[12,384,128]{2,1,0:T(8,128)(2,1)} %collective-permute-done.12.other_ref, ...), custom_call_target="tpu_custom_call" | custom-call | tf_op jit(solution)/shard_map/project/pallas_call | solution.py:358
  137.4 21.4 %all-to-all-done.2.bias_ref = bf16[128,24,384]{2,1,0:T(8,128)(2,1)S(1)} async-done(((bf16[128,24,384]{2,1,0:T(8,128)(2,1)}), bf16[128,24,384]{2,1,0:T(8,128)(2,1)S(1)}, u32[]{:S(2)}, u32[]{:S(2)}) %all-to-all-start.2) | async-done | bytes 2359328 | tf_op jit(solution)/shard_map/all_to_all | solution.py:34
  158.8 1.4 copy-done
  160.2 31.4 %attention.1 = bf16[12,384,128]{2,1,0:T(8,128)(2,1)} custom-call(bf16[12,384,128]{2,1,0:T(8,128)(2,1)} %get-tuple-element.31.q_ref, bf16[12,768,128]{2,1,0:T(8,128)(2,1)} %get-tuple-element.32.k_ref, bf16[12,4,48,768]{3,2,1,0:T(8,128)(2,1)} %get-tuple-element.33.vt_ref, f32[12,128,384]{2,1,0:T(8,128)} %get-tuple-element.34.gate_ref, ...), custom_call_target="tpu_custom_call" | custom-call | tf_op jit(solution)/shard_map/attention/pallas_call | solution.py:470
  191.5 1.3 copy.56
  192.9 23.2 %all_to_all.20 = bf16[16,6,48,128]{3,2,1,0:T(8,128)(2,1)S(1)} all-to-all(bf16[16,6,48,128]{3,2,1,0:T(8,128)(2,1)S(1)} %bitcast.53), channel_id=1, replica_groups=mesh['rh'=8,'core'=2,'col'=8] {'core','col'}, dimensions={0} | all-to-all | bytes 2359296 | tf_op jit(solution)/shard_map/all_to_all | solution.py:34
  216.1 1.1 copy.57
  (43 shorter events, 0.2 us)
Async XLA Ops:
  10.0 19.6 %copy-start.11 = (s32[48]{0:T(128)S(1)}, s32[48]{0:T(128)}, u32[]{:S(2)}) copy-start(s32[48]{0:T(128)} %param.18) | copy-start | bytes 580
  10.0 19.6 %copy-start.12 = (s32[48]{0:T(128)S(1)}, s32[48]{0:T(128)}, u32[]{:S(2)}) copy-start(s32[48]{0:T(128)} %param.17) | copy-start | bytes 580
  10.0 19.6 %copy-start.6 = (f32[3,48]{1,0:T(4,128)S(1)}, f32[3,48]{1,0:T(4,128)}, u32[]{:S(2)}) copy-start(f32[3,48]{1,0:T(4,128)} %param.16) | copy-start | bytes 1732
  10.0 21.3 %copy-start.5 = (f32[36,128]{1,0:T(8,128)S(1)}, f32[36,128]{1,0:T(8,128)}, u32[]{:S(2)}) copy-start(f32[36,128]{1,0:T(8,128)} %param.24) | copy-start | bytes 55300
  10.0 21.3 %copy-start.8 = (f32[128]{0:T(128)S(1)}, f32[128]{0:T(128)}, u32[]{:S(2)}) copy-start(f32[128]{0:T(128)} %param.25) | copy-start | bytes 1540
  10.0 55.0 %all-to-all-start = ((bf16[128,72,128]{2,1,0:T(8,128)(2,1)}), bf16[128,72,128]{2,1,0:T(8,128)(2,1)S(1)}, u32[]{:S(2)}, u32[]{:S(2)}) async-start(bf16[128,72,128]{2,1,0:T(8,128)(2,1)} %get-tuple-element.21), calls=%async_computation | async-start | bytes 4718592 | tf_op jit(solution)/shard_map/all_to_all | solution.py:34
  21.5 35.2 %collective-permute-start = (bf16[6,96,128]{2,1,0:T(8,128)(2,1)}, bf16[6,96,128]{2,1,0:T(8,128)(2,1)}, u32[]{:S(2)}, u32[]{:S(2)}) collective-permute-start(bf16[6,96,128]{2,1,0:T(8,128)(2,1)} %get-tuple-element.23), channel_id=1, source_target_pairs={{0,1},{1,2},{2,3},{3,4},{4,5},{5,6},{6,7},{7,0},{8,9},{9,10},{10,1... | collective-permute-start | bytes 442376 | tf_op jit(solution)/shard_map/ppermute | solution.py:526
  23.1 38.9 %collective-permute-start.1 = (bf16[6,96,128]{2,1,0:T(8,128)(2,1)}, bf16[6,96,128]{2,1,0:T(8,128)(2,1)}, u32[]{:S(2)}, u32[]{:S(2)}) collective-permute-start(bf16[6,96,128]{2,1,0:T(8,128)(2,1)} %get-tuple-element.24), channel_id=1, source_target_pairs={{0,2},{1,3},{2,4},{3,5},{4,6},{5,7},{6,0},{7,1},{8,10},{9,11},{10,... | collective-permute-start | bytes 442376 | tf_op jit(solution)/shard_map/ppermute | solution.py:526
  26.0 38.0 %collective-permute-start.2 = (bf16[6,96,128]{2,1,0:T(8,128)(2,1)}, bf16[6,96,128]{2,1,0:T(8,128)(2,1)}, u32[]{:S(2)}, u32[]{:S(2)}) collective-permute-start(bf16[6,96,128]{2,1,0:T(8,128)(2,1)} %get-tuple-element.25), channel_id=1, source_target_pairs={{0,3},{1,4},{2,5},{3,6},{4,7},{5,0},{6,1},{7,2},{8,11},{9,12},{10,... | collective-permute-start | bytes 442376 | tf_op jit(solution)/shard_map/ppermute | solution.py:526
  29.4 51.5 %collective-permute-start.3 = (bf16[6,96,128]{2,1,0:T(8,128)(2,1)}, bf16[6,96,128]{2,1,0:T(8,128)(2,1)}, u32[]{:S(2)}, u32[]{:S(2)}) collective-permute-start(bf16[6,96,128]{2,1,0:T(8,128)(2,1)} %get-tuple-element.26), channel_id=1, source_target_pairs={{0,4},{1,5},{2,6},{3,7},{4,0},{5,1},{6,2},{7,3},{8,12},{9,13},{10,... | collective-permute-start | bytes 442376 | tf_op jit(solution)/shard_map/ppermute | solution.py:526
  29.7 3.7 %collective-permute-start.8 = (f32[1,240]{1,0:T(1,128)S(1)}, f32[1,240]{1,0:T(1,128)S(1)}, u32[]{:S(2)}, u32[]{:S(2)}) collective-permute-start(f32[1,240]{1,0:T(1,128)S(1)} %reshape.82), channel_id=1, source_target_pairs={{0,8},{8,0},{16,24},{24,16},{32,40},{40,32},{48,56},{56,48},{64,72... | collective-permute-start | bytes 2888 | tf_op jit(solution)/shard_map/ppermute | solution.py:541
  33.4 48.5 %collective-permute-start.4 = (bf16[6,96,128]{2,1,0:T(8,128)(2,1)}, bf16[6,96,128]{2,1,0:T(8,128)(2,1)}, u32[]{:S(2)}, u32[]{:S(2)}) collective-permute-start(bf16[6,96,128]{2,1,0:T(8,128)(2,1)} %get-tuple-element.27), channel_id=1, source_target_pairs={{0,5},{1,6},{2,7},{3,0},{4,1},{5,2},{6,3},{7,4},{8,13},{9,14},{10,... | collective-permute-start | bytes 442376 | tf_op jit(solution)/shard_map/ppermute | solution.py:526
  56.7 26.1 %collective-permute-start.5 = (bf16[6,96,128]{2,1,0:T(8,128)(2,1)}, bf16[6,96,128]{2,1,0:T(8,128)(2,1)}, u32[]{:S(2)}, u32[]{:S(2)}) collective-permute-start(bf16[6,96,128]{2,1,0:T(8,128)(2,1)} %get-tuple-element.28), channel_id=1, source_target_pairs={{0,6},{1,7},{2,0},{3,1},{4,2},{5,3},{6,4},{7,5},{8,14},{9,15},{10,... | collective-permute-start | bytes 442376 | tf_op jit(solution)/shard_map/ppermute | solution.py:526
  61.9 21.8 %collective-permute-start.6 = (bf16[6,96,128]{2,1,0:T(8,128)(2,1)}, bf16[6,96,128]{2,1,0:T(8,128)(2,1)}, u32[]{:S(2)}, u32[]{:S(2)}) collective-permute-start(bf16[6,96,128]{2,1,0:T(8,128)(2,1)} %get-tuple-element.29), channel_id=1, source_target_pairs={{0,7},{1,0},{2,1},{3,2},{4,3},{5,4},{6,5},{7,6},{8,15},{9,8},{10,9... | collective-permute-start | bytes 442376 | tf_op jit(solution)/shard_map/ppermute | solution.py:526
  64.0 23.0 %collective-permute-start.9 = (f32[2,240]{1,0:T(2,128)S(1)}, f32[2,240]{1,0:T(2,128)S(1)}, u32[]{:S(2)}, u32[]{:S(2)}) collective-permute-start(f32[2,240]{1,0:T(2,128)S(1)} %pad_maximum_fusion.4), channel_id=1, source_target_pairs={{0,16},{8,24},{16,0},{24,8},{32,48},{40,56},{48,32},{56,40},{64,80... | collective-permute-start | bytes 5768 | tf_op jit(solution)/shard_map/ppermute | solution.py:541
  65.0 1.4 copy-start.1
  72.4 32.1 %all-to-all-start.1 = ((bf16[128,36,128]{2,1,0:T(8,128)(2,1)}), bf16[128,36,128]{2,1,0:T(8,128)(2,1)S(1)}, u32[]{:S(2)}, u32[]{:S(2)}) async-start(bf16[128,36,128]{2,1,0:T(8,128)(2,1)} %triangle.1), calls=%async_computation.1 | async-start | bytes 2621440 | tf_op jit(solution)/shard_map/all_to_all | solution.py:34
  84.7 3.0 %copy-start.10 = (s32[16]{0:T(128)S(1)}, s32[16]{0:T(128)}, u32[]{:S(2)}) copy-start(s32[16]{0:T(128)} %fusion.1) | copy-start | bytes 196
  84.7 16.1 %copy-start.9 = (f32[128]{0:T(128)S(1)}, f32[128]{0:T(128)}, u32[]{:S(2)}) copy-start(f32[128]{0:T(128)} %param.20) | copy-start | bytes 1540
  84.8 16.9 %copy-start.7 = (bf16[128,4]{0,1:T(4,128)(2,1)S(1)}, bf16[128,4]{0,1:T(4,128)(2,1)}, u32[]{:S(2)}) copy-start(bf16[128,4]{0,1:T(4,128)(2,1)} %param.28) | copy-start | bytes 3076
  85.9 18.7 %collective-permute-start.7 = (bf16[8,6,48,128]{3,2,1,0:T(8,128)(2,1)}, bf16[8,6,48,128]{3,2,1,0:T(8,128)(2,1)S(1)}, u32[]{:S(2)}, u32[]{:S(2)}) collective-permute-start(bf16[8,6,48,128]{3,2,1,0:T(8,128)(2,1)} %get-tuple-element.37), channel_id=1, source_target_pairs={{0,8},{8,0},{1,9},{9,1},{2,10},{10,2},{3,11},{11,3},{4,12},{12,4},... | collective-permute-start | bytes 1769480 | tf_op jit(solution)/shard_map/ppermute | solution.py:532
  87.0 9.5 %collective-permute-start.10 = (f32[4,240]{1,0:T(4,128)S(1)}, f32[4,240]{1,0:T(4,128)S(1)}, u32[]{:S(2)}, u32[]{:S(2)}) collective-permute-start(f32[4,240]{1,0:T(4,128)S(1)} %pad_maximum_fusion.3), channel_id=1, source_target_pairs={{0,32},{8,40},{16,48},{24,56},{32,0},{40,8},{48,16},{56,24},{64,96... | collective-permute-start | bytes 11528 | tf_op jit(solution)/shard_map/ppermute | solution.py:541
  96.5 5.8 %collective-permute-start.11 = (f32[8,240]{1,0:T(8,128)S(1)}, f32[8,240]{1,0:T(8,128)S(1)}, u32[]{:S(2)}, u32[]{:S(2)}) collective-permute-start(f32[8,240]{1,0:T(8,128)S(1)} %pad_maximum_fusion.1), channel_id=1, source_target_pairs={{0,64},{8,72},{16,80},{24,88},{32,96},{40,104},{48,112},{56,120},{... | collective-permute-start | bytes 23048 | tf_op jit(solution)/shard_map/ppermute | solution.py:541
  104.5 0.8 copy-start.4
  104.5 1.3 copy-start.2
  116.8 9.4 %copy-start.3 = (bf16[12,384,128]{2,1,0:T(8,128)(2,1)S(1)}, bf16[12,384,128]{2,1,0:T(8,128)(2,1)}, u32[]{:S(2)}) copy-start(bf16[12,384,128]{2,1,0:T(8,128)(2,1)} %get-tuple-element.30.own_ref) | copy-start | bytes 3538948
  116.8 42.0 %all-to-all-start.2 = ((bf16[128,24,384]{2,1,0:T(8,128)(2,1)}), bf16[128,24,384]{2,1,0:T(8,128)(2,1)S(1)}, u32[]{:S(2)}, u32[]{:S(2)}) async-start(bf16[128,24,384]{2,1,0:T(8,128)(2,1)} %bitcast.51), calls=%async_computation.2 | async-start | bytes 4718592 | tf_op jit(solution)/shard_map/all_to_all | solution.py:34
  126.2 5.5 %collective-permute-start.12 = (bf16[12,384,128]{2,1,0:T(8,128)(2,1)S(1)}, bf16[12,384,128]{2,1,0:T(8,128)(2,1)}, u32[]{:S(2)}, u32[]{:S(2)}) collective-permute-start(bf16[12,384,128]{2,1,0:T(8,128)(2,1)S(1)} %copy-done.3), channel_id=1, source_target_pairs={{0,8},{1,9},{2,10},{3,11},{4,12},{5,13},{6,14},{7,15},{8,0},{9,1},... | collective-permute-start | bytes 3538952 | tf_op jit(solution)/shard_map/ppermute | solution.py:576
  158.8 1.4 copy-start

commit v2 on v1

--- a/solution.py
+++ b/solution.py
@@ -177,6 +177,7 @@
             pltpu.VMEM((total, n_col * LANES), BF),
             pltpu.VMEM((total // LANES, total, LANES), F32),
         ],
+        compiler_params=pltpu.CompilerParams(vmem_limit_bytes=24 << 20),
         name="triangle",
     )(sides)
 
@@ -216,7 +217,7 @@
     n_pa = n_in // n_lt
     n_in8 = sc.shape[0] // ch
     n_col = keep_ref.shape[0]
-    n_heads = bias_ref.shape[1]
+    n_heads = bias_ref.shape[3] // two_ref.shape[0]
     tn = (((0,), (0,)), ((), ()))
 
     @pl.when(pl.program_id(0) == 0)
@@ -269,11 +270,14 @@
     )
     two = (pair.astype(F32) + gate * tri + binned).astype(BF)
     normed = (unit_norm(two, ones) * gain_attn_ref[...]).astype(BF)
-    bias = dot_nt(wbias_ref[...], normed)[:n_heads].astype(BF)
+    bias = dot_nt(wbias_ref[...], normed)[:n_heads]
     for v in range(n_row):
         two_ref[v] = two[v * n_q : (v + 1) * n_q]
         normed_ref[v] = normed[v * n_q : (v + 1) * n_q]
-        bias_ref[v] = bias[:, v * n_q : (v + 1) * n_q]
+    bias = jnp.concatenate([bias[:, v * n_q : (v + 1) * n_q] for v in range(n_row)], axis=0)
+    for g in range(bias_ref.shape[0]):
+        for c in range(n_col):
+            bias_ref[g, 0, c] = bias.astype(BF)
 
 
 def bin_weights(w_bins, same_chain):
@@ -284,13 +288,14 @@
     return jnp.concatenate([high, high, rows - high], axis=0).astype(BF)
 
 
-def update(place, back, keep, other, near, far, gains, wgo, wout, wbins, wbias_t, n_heads, n_bins, n_row=6):
+def update(sizes, place, back, keep, other, near, far, gains, wgo, wout, wbins, wbias_t, n_heads, n_bins):
     ch, n_in, _ = back.shape
     n_col, sub, half, _ = keep.shape
     n_q = n_col * half
-    n_pa = 2 * sub
+    n_rh, n_core, _ = sizes
+    n_pa = n_core * sub
+    n_row = sub
     n_in8 = -(-n_in // 8) * 8
-    per = sub // n_row
     fixed = lambda i: (0, 0)
     row = lambda i: (i, 0, 0)
     return pl.pallas_call(
@@ -299,8 +304,8 @@
         in_specs=[
             pl.BlockSpec(memory_space=pltpu.SMEM),
             pl.BlockSpec(back.shape, lambda i: (0, 0, 0)),
-            pl.BlockSpec((n_col, n_row, half, ch), lambda i: (0, i % per, 0, 0)),
-            pl.BlockSpec((n_col, n_row, half, ch), lambda i: (0, i % per, 0, 0)),
+            pl.BlockSpec((n_col, n_row, half, ch), lambda i: (0, 0, 0, 0)),
+            pl.BlockSpec((n_col, n_row, half, ch), lambda i: (0, 0, 0, 0)),
             pl.BlockSpec(memory_space=pltpu.SMEM),
             pl.BlockSpec(far.shape, fixed),
             pl.BlockSpec((1, ch), fixed),
@@ -314,12 +319,14 @@
         out_specs=[
             pl.BlockSpec((n_row, n_q, ch), row),
             pl.BlockSpec((n_row, n_q, ch), row),
-            pl.BlockSpec((n_row, n_heads, n_q), row),
+            pl.BlockSpec(
+                (n_rh, 1, n_col, sub * n_heads, n_q), lambda i: (0, i, 0, 0, 0)
+            ),
         ],
         out_shape=[
             jax.ShapeDtypeStruct((n_pa, n_q, ch), BF),
             jax.ShapeDtypeStruct((n_pa, n_q, ch), BF),
-            jax.ShapeDtypeStruct((n_pa, n_heads, n_q), BF),
+            jax.ShapeDtypeStruct((n_rh, n_core, n_col, sub * n_heads, n_q), BF),
         ],
         scratch_shapes=[pltpu.VMEM((ch * n_in8, LANES), F32)],
         name="update",
@@ -384,7 +391,7 @@
 
 
 def attention_kernel(
-    sub, q_ref, k_ref, vt_ref, gate_ref, two_ref, bias_ref, wo_ref, out_ref, raw_sc, bias_sc
+    q_ref, k_ref, vt_ref, gate_ref, two_ref, bias_ref, wo_ref, out_ref, raw_sc, bias_sc
 ):
     n_unit, n_k, _ = bias_sc.shape
     n_q, ch = q_ref.shape[1:]
@@ -393,7 +400,8 @@
     n_src, n_pay, _ = bias_ref.shape
     n_lt = n_q // LANES
     n_rh = n_src // 16
-    n_col = n_q // sub // n_rh
+    n_col, _, half, _ = out_ref.shape[1:]
+    sub = n_q // n_rh // n_col
     pairs = n_heads // 2
 
     @pl.when(pl.program_id(0) == 0)
@@ -454,22 +462,30 @@
                 res = lax.dot_general(
                     gated, wo_ref[...], (((0,), (0,)), ((), ())), preferred_element_type=F32
                 )
-                out_ref[r, cols, :] = (two_ref[r, cols, :].astype(F32) + res).astype(BF)
+                res = (two_ref[r, cols, :].astype(F32) + res).astype(BF)
+                at = t * LANES
+                while at < (t + 1) * LANES:
+                    c, off = divmod(at, half)
+                    size = min(half - off, (t + 1) * LANES - at)
+                    out_ref[0, c, r, off : off + size] = res[at - t * LANES : at - t * LANES + size]
+                    at += size
             s = ahead
         return carry
 
-    lax.fori_loop(0, q_ref.shape[0], row, 0, unroll=2)
-
-
-def attention(q, k, vt, gate, two, bias, wo, sub, n_row=2):
+    lax.fori_loop(0, q_ref.shape[0], row, 0)
+
+
+def attention(q, k, vt, gate, two, bias, wo, n_col, n_row=3):
     n_rows, n_q, ch = q.shape
     n_src, n_pay, _ = bias.shape
     n_heads = vt.shape[1]
     n_lt = n_q // LANES
+    half = n_q // n_col
+    steps = n_rows // 2 // n_row
     row = lambda i: (i, 0, 0)
     return pl.pallas_call(
-        functools.partial(attention_kernel, sub),
-        grid=(n_rows // n_row,),
+        attention_kernel,
+        grid=(2 * steps,),
         in_specs=[
             pl.BlockSpec((n_row, n_q, ch), row),
             pl.BlockSpec((n_row, 2 * n_q, ch), row),
@@ -479,8 +495,10 @@
             pl.BlockSpec(bias.shape, lambda i: (0, 0, 0)),
             pl.BlockSpec(wo.shape, lambda i: (0, 0)),
         ],
-        out_specs=pl.BlockSpec((n_row, n_q, ch), row),
-        out_shape=jax.ShapeDtypeStruct(q.shape, BF),
+        out_specs=pl.BlockSpec(
+            (1, n_col, n_row, half, ch), lambda i: (i // steps, 0, i % steps, 0, 0)
+        ),
+        out_shape=jax.ShapeDtypeStruct((2, n_col, n_rows // 2, half, ch), BF),
         scratch_shapes=[
             pltpu.VMEM((n_lt, n_src * n_pay, LANES), F32),
             pltpu.VMEM((n_lt * n_heads // 2, 2 * n_q, 2 * LANES), F32),
@@ -518,6 +536,13 @@
     n_pa = n_core * sub
     n_q = n_col * half
 
+    packed = jnp.concatenate(
+        [coords, chain_ids.astype(F32)[None], coord_mask.astype(F32)[None]], axis=0
+    )
+    packed = jnp.broadcast_to(packed, (n_rh * n_core, *packed.shape))
+    known = exchange(packed, ("rh", "core"))
+    known = known.reshape(n_rh, n_core, -1, row_count)
+
     w_sides = w_tri_in[:, : 4 * ch].T
     sides, *pieces = make_sides(col.reshape(1), pair_in, gain_tri, w_sides, n_col)
     sides = exchange(sides, every)
@@ -531,17 +556,6 @@
     give = lax.dynamic_index_in_dim(whole, 1 - core, 2, keepdims=False)
     other_pair = lax.ppermute(give, "core", [(0, 1), (1, 0)])
 
-    packed = jnp.concatenate(
-        [coords, chain_ids.astype(F32)[None], coord_mask.astype(F32)[None]], axis=0
-    ).reshape(1, -1)
-    n_row = n_rh * n_core
-    step = 1
-    while step < n_row:
-        swap = [(r, r ^ step) for r in range(n_row)]
-        packed = jnp.concatenate([packed, lax.ppermute(packed, ("rh", "core"), swap)], axis=0)
-        step *= 2
-    at = jnp.arange(n_row) ^ (rh * n_core + core)
-    known = packed[at].reshape(n_rh, n_core, -1, row_count)
     near = lax.dynamic_index_in_dim(known, rh, 0, keepdims=False)
     near = near.transpose(1, 0, 2).reshape(-1, n_core, sub, n_col)
     near = lax.dynamic_index_in_dim(near, col, 3, keepdims=False).reshape(-1, n_pa)
@@ -551,6 +565,7 @@
     product = triangle(sides, n_rh, n_core, n_col, row_count, col_count)
     back = exchange(product, every)
     two, normed, bias = update(
+        (n_rh, n_core, n_col),
         jnp.stack([core, col]),
         back,
         keep,
@@ -566,13 +581,7 @@
         n_bins,
     )
 
-    n_pay = sub * n_heads
-    spread = exchange(
-        jnp.broadcast_to(
-            bias.reshape(1, n_core, 1, n_pay, n_q), (n_rh, n_core, n_col, n_pay, n_q)
-        ).reshape(n_dev, n_pay, n_q),
-        every,
-    )
+    spread = exchange(bias.reshape(n_dev, sub * n_heads, n_q), every)
     other = lax.ppermute(normed, every, [(d, d ^ n_col) for d in range(n_dev)])
     q, k, v_t, gate = project(
         core.reshape(1),
@@ -584,13 +593,8 @@
         w_attn[:, 2 * ch :].T,
         n_heads,
     )
-    result = attention(q, k, v_t, gate, two, spread, w_attn_out, sub)
-    home = exchange(
-        result.reshape(n_core, sub, n_col, half, ch)
-        .transpose(0, 2, 1, 3, 4)
-        .reshape(n_core * n_col, sub, half, ch),
-        ("core", "col"),
-    )
+    result = attention(q, k, v_t, gate, two, spread, w_attn_out, n_col)
+    home = exchange(result.reshape(n_core * n_col, sub, half, ch), ("core", "col"))
     return (
         home.reshape(n_core, n_col, sub, half, ch)
         .transpose(2, 1, 0, 3, 4)

time: 218 us -> 212 us (0.972)
  starting transfers between devices: 53 us -> 47.9 us
  local copies, waits for them, and re-layouts: 28.8 us -> 26.4 us
    all_to_all x3 -> x4, waiting for transfers between devices: 21.4 us -> 30.5 us  [exchange(): return lax.all_to_all(x, axes, split_axis=0, concat_axis=0, tiled=True)]
    ppermute x4 -> x0, waiting for transfers between devices: 8.72 us -> none  [body(): lax.ppermute(packed, ('rh', 'core'), swap)]
    ppermute x4 -> x0, starting transfers between devices: 4.84 us -> none  [body(): lax.ppermute(packed, ('rh', 'core'), swap)]
    pallas_call x1, Pallas kernels: 6 us -> 3.26 us  [triangle(): pl.pallas_call(functools.partial(triangle_kernel, n_rh, n_core, n_col, n_...]
    all_to_all x3 -> x4, starting transfers between devices: 29.4 us -> 28.9 us  [exchange(): return lax.all_to_all(x, axes, split_axis=0, concat_axis=0, tiled=True)]
  transfers between devices with their start and end apart: 16 -> 13, of which waited for: 3 -> 4; matrix products, arithmetic and copies ran while one was open for 9% -> 10% of each run, Pallas kernels for 5% -> 4%
where the time goes in v2:
time: 212 us; the launch traced here: 211 us
  Pallas kernels  59.3 us (28%)
  waiting for transfers between devices  51.4 us (24%)
  starting transfers between devices  47.9 us (23%)
  local copies, waits for them, and re-layouts  26.4 us (12%)
  blocking collectives  24.3 us (11%)
    pallas_call x1, Pallas kernels, attention(): pl.pallas_call(attention_kernel, grid=(2 * steps,), in_specs=[pl.BlockSpe...  33.1 us
    all_to_all x4, waiting for transfers between devices, exchange(): return lax.all_to_all(x, axes, split_axis=0, concat_axis=0, tiled=True)  30.5 us
    all_to_all x4, starting transfers between devices, exchange(): return lax.all_to_all(x, axes, split_axis=0, concat_axis=0, tiled=True)  28.9 us
    all_to_all x1, blocking collectives, exchange(): return lax.all_to_all(x, axes, split_axis=0, concat_axis=0, tiled=True)  24.3 us
    ppermute x7, waiting for transfers between devices, body(): lax.ppermute(pieces[d], 'col', [(i, (i + d) % n_col) for i in range(n_col)])  20.9 us
    ppermute x7, starting transfers between devices, body(): lax.ppermute(pieces[d], 'col', [(i, (i + d) % n_col) for i in range(n_col)])  16.5 us
    unnamed x36, local copies, waits for them, and re-layouts  15.4 us
    pallas_call x1, Pallas kernels, update(): pl.pallas_call(functools.partial(update_kernel, n_bins), grid=(n_pa // n_...  9.03 us
  transfers between devices with their start and end apart: 13, of which 4 were waited for; matrix products, arithmetic and copies ran while one was open for 10% of the time, Pallas kernels for 4%

profile of v2, /device:TPU:1, one launch (start us, length us, event | category | flops | bytes accessed | tf_op | source)
XLA Modules:
  0.0 211.4 jit_solution(2555664024939468477)
XLA Ops:
  0.0 0.9 slice.15
  0.9 0.8 copy.70
  1.7 8.3 %sides.1 = (bf16[128,72,128]{2,1,0:T(8,128)(2,1)}, bf16[6,96,128]{2,1,0:T(8,128)(2,1)}, bf16[6,96,128]{2,1,0:T(8,128)(2,1)}, bf16[6,96,128]{2,1,0:T(8,128)(2,1)}...) custom-call(s32[1]{0:T(128)} %bitcast.1.col_ref, ...), custom_call_target="tpu_custom_call" | custom-call | tf_op jit(solution)/shard_map/sides/pallas_call | solution.py:105
  10.0 11.5 %all-to-all-start = ((bf16[128,72,128]{2,1,0:T(8,128)(2,1)}), bf16[128,72,128]{2,1,0:T(8,128)(2,1)S(1)}, u32[]{:S(2)}, u32[]{:S(2)}) async-start(bf16[128,72,128]{2,1,0:T(8,128)(2,1)} %get-tuple-element.21), calls=%async_computation | async-start | bytes 4718592 | tf_op jit(solution)/shard_map/all_to_all | solution.py:34
  21.5 1.6 collective-permute-start
  23.0 2.9 %collective-permute-start.1 = (bf16[6,96,128]{2,1,0:T(8,128)(2,1)}, bf16[6,96,128]{2,1,0:T(8,128)(2,1)}, u32[]{:S(2)}, u32[]{:S(2)}) collective-permute-start(bf16[6,96,128]{2,1,0:T(8,128)(2,1)} %get-tuple-element.24), channel_id=1, source_target_pairs={{0,2},{1,3},{2,4},{3,5},{4,6},{5,7},{6,0},{7,1},{8,10},{9,11},{10,... | collective-permute-start | bytes 442376 | tf_op jit(solution)/shard_map/ppermute | solution.py:551
  25.9 3.5 %collective-permute-start.2 = (bf16[6,96,128]{2,1,0:T(8,128)(2,1)}, bf16[6,96,128]{2,1,0:T(8,128)(2,1)}, u32[]{:S(2)}, u32[]{:S(2)}) collective-permute-start(bf16[6,96,128]{2,1,0:T(8,128)(2,1)} %get-tuple-element.25), channel_id=1, source_target_pairs={{0,3},{1,4},{2,5},{3,6},{4,7},{5,0},{6,1},{7,2},{8,11},{9,12},{10,... | collective-permute-start | bytes 442376 | tf_op jit(solution)/shard_map/ppermute | solution.py:551
  29.4 0.1 collective-permute-start.3
  29.5 3.1 %collective-permute-start.4 = (bf16[6,96,128]{2,1,0:T(8,128)(2,1)}, bf16[6,96,128]{2,1,0:T(8,128)(2,1)}, u32[]{:S(2)}, u32[]{:S(2)}) collective-permute-start(bf16[6,96,128]{2,1,0:T(8,128)(2,1)} %get-tuple-element.27), channel_id=1, source_target_pairs={{0,5},{1,6},{2,7},{3,0},{4,1},{5,2},{6,3},{7,4},{8,13},{9,14},{10,... | collective-permute-start | bytes 442376 | tf_op jit(solution)/shard_map/ppermute | solution.py:551
  32.6 0.9 constant_dynamic-update-slice_fusion.7
  33.6 0.6 broadcast_in_dim.14
  34.2 1.5 reshape.69
  35.8 20.9 %collective-permute-done = bf16[6,96,128]{2,1,0:T(8,128)(2,1)} collective-permute-done((bf16[6,96,128]{2,1,0:T(8,128)(2,1)}, bf16[6,96,128]{2,1,0:T(8,128)(2,1)}, u32[]{:S(2)}, u32[]{:S(2)}) %collective-permute-start) | collective-permute-done | bytes 147488 | tf_op jit(solution)/shard_map/ppermute | solution.py:551
  56.7 4.3 %collective-permute-start.5 = (bf16[6,96,128]{2,1,0:T(8,128)(2,1)}, bf16[6,96,128]{2,1,0:T(8,128)(2,1)}, u32[]{:S(2)}, u32[]{:S(2)}) collective-permute-start(bf16[6,96,128]{2,1,0:T(8,128)(2,1)} %get-tuple-element.28), channel_id=1, source_target_pairs={{0,6},{1,7},{2,0},{3,1},{4,2},{5,3},{6,4},{7,5},{8,14},{9,15},{10,... | collective-permute-start | bytes 442376 | tf_op jit(solution)/shard_map/ppermute | solution.py:551
  60.9 0.9 constant_dynamic-update-slice_fusion.6
  61.9 0.0 collective-permute-done.1
  61.9 1.1 collective-permute-start.6
  63.0 0.9 constant_dynamic-update-slice_fusion.5
  63.9 0.0 all-to-all-done.in_ref
  63.9 4.7 %all-to-all-start.2 = ((f32[16,1,240]{2,1,0:T(1,128)}), f32[16,1,240]{2,1,0:T(1,128)S(1)}, u32[]{:S(2)}, u32[]{:S(2)}) async-start(f32[16,1,240]{2,1,0:T(1,128)} %reshape.69), calls=%async_computation.2 | async-start | bytes 32768 | tf_op jit(solution)/shard_map/all_to_all | solution.py:34
  68.6 0.0 collective-permute-done.2
  68.6 0.9 constant_dynamic-update-slice_fusion.4
  69.5 3.3 %triangle.1 = bf16[128,36,128]{2,1,0:T(8,128)(2,1)S(1)} custom-call(bf16[128,72,128]{2,1,0:T(8,128)(2,1)S(1)} %all-to-all-done.in_ref), custom_call_target="tpu_custom_call" | custom-call | tf_op jit(solution)/shard_map/triangle/pallas_call | solution.py:172
  72.8 1.1 copy-done
  73.9 0.5 all-to-all-done.2
  74.4 7.7 %all-to-all-start.1 = ((bf16[128,36,128]{2,1,0:T(8,128)(2,1)}), bf16[128,36,128]{2,1,0:T(8,128)(2,1)S(1)}, u32[]{:S(2)}, u32[]{:S(2)}) async-start(bf16[128,36,128]{2,1,0:T(8,128)(2,1)} %copy-done), calls=%async_computation.1 | async-start | bytes 2621440 | tf_op jit(solution)/shard_map/all_to_all | solution.py:34
  82.0 0.0 collective-permute-done.3
  82.1 0.9 constant_dynamic-update-slice_fusion.3
  83.0 0.9 constant_dynamic-update-slice_fusion.2
  83.9 0.9 constant_dynamic-update-slice_fusion.1
  84.9 0.9 constant_dynamic-update-slice_fusion
  85.8 0.0 copy-start.8
  85.8 0.0 copy-start.7
  85.9 0.0 copy-start.5
  85.9 0.0 copy-start.9
  85.9 1.1 dynamic-slice_bitcast_fusion
  87.0 1.1 collective-permute-start.7
  88.1 1.4 slice.16.wgo_ref
  89.4 0.7 copy.65.gain_sum_ref
  90.2 0.6 pad.9.wbias_ref
  90.8 0.6 pad_add_fusion.place_ref
  91.4 0.6 pad_maximum_fusion.wbins_ref
  92.0 0.5 broadcast.13
  92.5 0.6 reduce.2
  93.1 0.1 reshape.70
  93.2 0.7 reshape.61.far_ref
  93.8 0.1 reshape.59
  93.9 0.2 dynamic-slice_reduce_fusion
  94.1 0.7 reshape.60.near_ref
  94.8 8.8 %all-to-all-done.1.back_ref = bf16[128,36,128]{2,1,0:T(8,128)(2,1)S(1)} async-done(((bf16[128,36,128]{2,1,0:T(8,128)(2,1)}), bf16[128,36,128]{2,1,0:T(8,128)(2,1)S(1)}, u32[]{:S(2)}, u32[]{:S(2)}) %all-to-all-start.1) | async-done | bytes 1179680 | tf_op jit(solution)/shard_map/all_to_all | solution.py:34
  103.6 1.1 copy-done.2
  104.7 9.0 %update.1 = (bf16[12,384,128]{2,1,0:T(8,128)(2,1)}, bf16[12,384,128]{2,1,0:T(8,128)(2,1)}, bf16[8,2,8,24,384]{4,3,2,1,0:T(8,128)(2,1)}) custom-call(s32[2]{0:T(128)} %pad_add_fusion.place_ref, bf16[128,36,128]{2,1,0:T(8,128)(2,1)} %copy-done.2, bf16[8,6,48,128]{3,2,1,0:T(8,128)(2,1)} %get-tuple-element.38.keep_ref, bf16[8,6,48,128]{3,2,1,0:T(8,128)(2,1)} %copy-done.4, ...), custom_call_target="tpu_custom_call" | custom-call | tf_op jit(solution)/shard_map/update/pallas_call | solution.py:301
  113.7 5.1 %all-to-all-start.3 = ((bf16[128,24,384]{2,1,0:T(8,128)(2,1)}), bf16[128,24,384]{2,1,0:T(8,128)(2,1)S(1)}, u32[]{:S(2)}, u32[]{:S(2)}) async-start(bf16[128,24,384]{2,1,0:T(8,128)(2,1)} %bitcast.46), calls=%async_computation.3 | async-start | bytes 4718592 | tf_op jit(solution)/shard_map/all_to_all | solution.py:34
  118.8 1.5 collective-permute-start.8
  120.3 1.4 fusion.1
  121.7 1.5 copy.74
  123.2 1.5 copy.73
  124.7 0.0 collective-permute-done.8.other_ref
  124.7 5.7 %project.1 = (bf16[12,384,128]{2,1,0:T(8,128)(2,1)}, bf16[12,768,128]{2,1,0:T(8,128)(2,1)}, bf16[12,4,48,768]{3,2,1,0:T(8,128)(2,1)}, f32[12,128,384]{2,1,0:T(8,128)}) custom-call(s32[1]{0:T(128)} %bitcast.core_ref, bf16[12,384,128]{2,1,0:T(8,128)(2,1)} %get-tuple-element.30.own_ref, bf16[12,384,128]{2,1,0:T(8,128)(2,1)} %collective-permute-done.8.other_ref, ...), custom_call_target="tpu_custom_call" | custom-call | tf_op jit(solution)/shard_map/project/pallas_call | solution.py:365
  130.3 21.2 %all-to-all-done.3.bias_ref = bf16[128,24,384]{2,1,0:T(8,128)(2,1)S(1)} async-done(((bf16[128,24,384]{2,1,0:T(8,128)(2,1)}), bf16[128,24,384]{2,1,0:T(8,128)(2,1)S(1)}, u32[]{:S(2)}, u32[]{:S(2)}) %all-to-all-start.3) | async-done | bytes 2359328 | tf_op jit(solution)/shard_map/all_to_all | solution.py:34
  151.6 1.4 copy-done.1
  153.0 33.1 %attention.1 = bf16[2,8,6,48,128]{4,3,2,1,0:T(8,128)(2,1)} custom-call(bf16[12,384,128]{2,1,0:T(8,128)(2,1)} %get-tuple-element.31.q_ref, bf16[12,768,128]{2,1,0:T(8,128)(2,1)} %get-tuple-element.32.k_ref, bf16[12,4,48,768]{3,2,1,0:T(8,128)(2,1)} %get-tuple-element.33.vt_ref, f32[12,128,384]{2,1,0:T(8,128)} %get-tuple-element.34.gate_ref, ...), custom_call_target="tpu_custom_call" | custom-call | tf_op jit(solution)/shard_map/attention/pallas_call | solution.py:486
  186.0 24.3 %all_to_all.25 = bf16[16,6,48,128]{3,2,1,0:T(8,128)(2,1)S(1)} all-to-all(bf16[16,6,48,128]{3,2,1,0:T(8,128)(2,1)} %bitcast.44), channel_id=1, replica_groups=mesh['rh'=8,'core'=2,'col'=8] {'core','col'}, dimensions={0} | all-to-all | bytes 2359296 | tf_op jit(solution)/shard_map/all_to_all | solution.py:34
  210.3 1.1 copy.68
  (27 shorter events, 0.1 us)
Async XLA Ops:
  10.0 22.7 %copy-start.10 = (s32[48]{0:T(128)S(1)}, s32[48]{0:T(128)}, u32[]{:S(2)}) copy-start(s32[48]{0:T(128)} %param.18) | copy-start | bytes 580
  10.0 22.7 %copy-start.11 = (s32[48]{0:T(128)S(1)}, s32[48]{0:T(128)}, u32[]{:S(2)}) copy-start(s32[48]{0:T(128)} %param.17) | copy-start | bytes 580
  10.0 23.6 %copy-start.6 = (f32[3,48]{1,0:T(4,128)S(1)}, f32[3,48]{1,0:T(4,128)}, u32[]{:S(2)}) copy-start(f32[3,48]{1,0:T(4,128)} %param.16) | copy-start | bytes 1732
  10.0 53.9 %all-to-all-start = ((bf16[128,72,128]{2,1,0:T(8,128)(2,1)}), bf16[128,72,128]{2,1,0:T(8,128)(2,1)S(1)}, u32[]{:S(2)}, u32[]{:S(2)}) async-start(bf16[128,72,128]{2,1,0:T(8,128)(2,1)} %get-tuple-element.21), calls=%async_computation | async-start | bytes 4718592 | tf_op jit(solution)/shard_map/all_to_all | solution.py:34
  21.5 35.2 %collective-permute-start = (bf16[6,96,128]{2,1,0:T(8,128)(2,1)}, bf16[6,96,128]{2,1,0:T(8,128)(2,1)}, u32[]{:S(2)}, u32[]{:S(2)}) collective-permute-start(bf16[6,96,128]{2,1,0:T(8,128)(2,1)} %get-tuple-element.23), channel_id=1, source_target_pairs={{0,1},{1,2},{2,3},{3,4},{4,5},{5,6},{6,7},{7,0},{8,9},{9,10},{10,1... | collective-permute-start | bytes 442376 | tf_op jit(solution)/shard_map/ppermute | solution.py:551
  23.0 38.9 %collective-permute-start.1 = (bf16[6,96,128]{2,1,0:T(8,128)(2,1)}, bf16[6,96,128]{2,1,0:T(8,128)(2,1)}, u32[]{:S(2)}, u32[]{:S(2)}) collective-permute-start(bf16[6,96,128]{2,1,0:T(8,128)(2,1)} %get-tuple-element.24), channel_id=1, source_target_pairs={{0,2},{1,3},{2,4},{3,5},{4,6},{5,7},{6,0},{7,1},{8,10},{9,11},{10,... | collective-permute-start | bytes 442376 | tf_op jit(solution)/shard_map/ppermute | solution.py:551
  25.9 42.7 %collective-permute-start.2 = (bf16[6,96,128]{2,1,0:T(8,128)(2,1)}, bf16[6,96,128]{2,1,0:T(8,128)(2,1)}, u32[]{:S(2)}, u32[]{:S(2)}) collective-permute-start(bf16[6,96,128]{2,1,0:T(8,128)(2,1)} %get-tuple-element.25), channel_id=1, source_target_pairs={{0,3},{1,4},{2,5},{3,6},{4,7},{5,0},{6,1},{7,2},{8,11},{9,12},{10,... | collective-permute-start | bytes 442376 | tf_op jit(solution)/shard_map/ppermute | solution.py:551
  29.4 52.7 %collective-permute-start.3 = (bf16[6,96,128]{2,1,0:T(8,128)(2,1)}, bf16[6,96,128]{2,1,0:T(8,128)(2,1)}, u32[]{:S(2)}, u32[]{:S(2)}) collective-permute-start(bf16[6,96,128]{2,1,0:T(8,128)(2,1)} %get-tuple-element.26), channel_id=1, source_target_pairs={{0,4},{1,5},{2,6},{3,7},{4,0},{5,1},{6,2},{7,3},{8,12},{9,13},{10,... | collective-permute-start | bytes 442376 | tf_op jit(solution)/shard_map/ppermute | solution.py:551
  29.5 53.5 %collective-permute-start.4 = (bf16[6,96,128]{2,1,0:T(8,128)(2,1)}, bf16[6,96,128]{2,1,0:T(8,128)(2,1)}, u32[]{:S(2)}, u32[]{:S(2)}) collective-permute-start(bf16[6,96,128]{2,1,0:T(8,128)(2,1)} %get-tuple-element.27), channel_id=1, source_target_pairs={{0,5},{1,6},{2,7},{3,0},{4,1},{5,2},{6,3},{7,4},{8,13},{9,14},{10,... | collective-permute-start | bytes 442376 | tf_op jit(solution)/shard_map/ppermute | solution.py:551
  56.7 27.3 %collective-permute-start.5 = (bf16[6,96,128]{2,1,0:T(8,128)(2,1)}, bf16[6,96,128]{2,1,0:T(8,128)(2,1)}, u32[]{:S(2)}, u32[]{:S(2)}) collective-permute-start(bf16[6,96,128]{2,1,0:T(8,128)(2,1)} %get-tuple-element.28), channel_id=1, source_target_pairs={{0,6},{1,7},{2,0},{3,1},{4,2},{5,3},{6,4},{7,5},{8,14},{9,15},{10,... | collective-permute-start | bytes 442376 | tf_op jit(solution)/shard_map/ppermute | solution.py:551
  61.9 23.0 %collective-permute-start.6 = (bf16[6,96,128]{2,1,0:T(8,128)(2,1)}, bf16[6,96,128]{2,1,0:T(8,128)(2,1)}, u32[]{:S(2)}, u32[]{:S(2)}) collective-permute-start(bf16[6,96,128]{2,1,0:T(8,128)(2,1)} %get-tuple-element.29), channel_id=1, source_target_pairs={{0,7},{1,0},{2,1},{3,2},{4,3},{5,4},{6,5},{7,6},{8,15},{9,8},{10,9... | collective-permute-start | bytes 442376 | tf_op jit(solution)/shard_map/ppermute | solution.py:551
  63.9 10.5 %all-to-all-start.2 = ((f32[16,1,240]{2,1,0:T(1,128)}), f32[16,1,240]{2,1,0:T(1,128)S(1)}, u32[]{:S(2)}, u32[]{:S(2)}) async-start(f32[16,1,240]{2,1,0:T(1,128)} %reshape.69), calls=%async_computation.2 | async-start | bytes 32768 | tf_op jit(solution)/shard_map/all_to_all | solution.py:34
  72.8 1.1 copy-start
  74.4 29.2 %all-to-all-start.1 = ((bf16[128,36,128]{2,1,0:T(8,128)(2,1)}), bf16[128,36,128]{2,1,0:T(8,128)(2,1)S(1)}, u32[]{:S(2)}, u32[]{:S(2)}) async-start(bf16[128,36,128]{2,1,0:T(8,128)(2,1)} %copy-done), calls=%async_computation.1 | async-start | bytes 2621440 | tf_op jit(solution)/shard_map/all_to_all | solution.py:34
  85.8 3.6 %copy-start.8 = (f32[128]{0:T(128)S(1)}, f32[128]{0:T(128)}, u32[]{:S(2)}) copy-start(f32[128]{0:T(128)} %param.20) | copy-start | bytes 1540
  85.8 4.3 %copy-start.7 = (bf16[128,4]{0,1:T(4,128)(2,1)S(1)}, bf16[128,4]{0,1:T(4,128)(2,1)}, u32[]{:S(2)}) copy-start(bf16[128,4]{0,1:T(4,128)(2,1)} %param.28) | copy-start | bytes 3076
  85.9 5.5 %copy-start.5 = (f32[36,128]{1,0:T(8,128)S(1)}, f32[36,128]{1,0:T(8,128)}, u32[]{:S(2)}) copy-start(f32[36,128]{1,0:T(8,128)} %param.24) | copy-start | bytes 55300
  85.9 5.5 %copy-start.9 = (f32[128]{0:T(128)S(1)}, f32[128]{0:T(128)}, u32[]{:S(2)}) copy-start(f32[128]{0:T(128)} %param.25) | copy-start | bytes 1540
  87.0 7.8 %collective-permute-start.7 = (bf16[8,6,48,128]{3,2,1,0:T(8,128)(2,1)}, bf16[8,6,48,128]{3,2,1,0:T(8,128)(2,1)S(1)}, u32[]{:S(2)}, u32[]{:S(2)}) collective-permute-start(bf16[8,6,48,128]{3,2,1,0:T(8,128)(2,1)} %get-tuple-element.37), channel_id=1, source_target_pairs={{0,8},{8,0},{1,9},{9,1},{2,10},{10,2},{3,11},{11,3},{4,12},{12,4},... | collective-permute-start | bytes 1769480 | tf_op jit(solution)/shard_map/ppermute | solution.py:557
  94.8 8.8 %copy-start.4 = (bf16[8,6,48,128]{3,2,1,0:T(8,128)(2,1)}, bf16[8,6,48,128]{3,2,1,0:T(8,128)(2,1)S(1)}, u32[]{:S(2)}) copy-start(bf16[8,6,48,128]{3,2,1,0:T(8,128)(2,1)S(1)} %collective-permute-done.7.other_ref) | copy-start | bytes 1769476
  103.6 1.1 copy-start.2
  113.7 5.1 %copy-start.3 = (bf16[12,384,128]{2,1,0:T(8,128)(2,1)S(1)}, bf16[12,384,128]{2,1,0:T(8,128)(2,1)}, u32[]{:S(2)}) copy-start(bf16[12,384,128]{2,1,0:T(8,128)(2,1)} %get-tuple-element.30.own_ref) | copy-start | bytes 3538948
  113.7 37.8 %all-to-all-start.3 = ((bf16[128,24,384]{2,1,0:T(8,128)(2,1)}), bf16[128,24,384]{2,1,0:T(8,128)(2,1)S(1)}, u32[]{:S(2)}, u32[]{:S(2)}) async-start(bf16[128,24,384]{2,1,0:T(8,128)(2,1)} %bitcast.46), calls=%async_computation.3 | async-start | bytes 4718592 | tf_op jit(solution)/shard_map/all_to_all | solution.py:34
  118.8 5.8 %collective-permute-start.8 = (bf16[12,384,128]{2,1,0:T(8,128)(2,1)S(1)}, bf16[12,384,128]{2,1,0:T(8,128)(2,1)}, u32[]{:S(2)}, u32[]{:S(2)}) collective-permute-start(bf16[12,384,128]{2,1,0:T(8,128)(2,1)S(1)} %copy-done.3), channel_id=1, source_target_pairs={{0,8},{1,9},{2,10},{3,11},{4,12},{5,13},{6,14},{7,15},{8,0},{9,1},... | collective-permute-start | bytes 3538952 | tf_op jit(solution)/shard_map/ppermute | solution.py:585
  151.6 1.4 copy-start.1

commit v3 on v2

--- a/solution.py
+++ b/solution.py
@@ -114,7 +114,7 @@
     )(col, pair, gain.reshape(1, ch), w_t)
 
 
-def triangle_kernel(n_rh, n_core, n_col, n_rows, n_cols, in_ref, out_ref, l_sc, r_sc, p_sc):
+def triangle_kernel(n_rh, n_core, n_col, n_rows, n_cols, in_ref, table_ref, out_ref, l_sc, r_sc, p_sc):
     third = n_rows // 3
     cut = LANES - n_cols
     total = n_rh * n_core * n_rows
@@ -165,12 +165,13 @@
     lax.fori_loop(0, n_rh, pack, 0)
 
 
-def triangle(sides, n_rh, n_core, n_col, n_rows, n_cols):
+def triangle(sides, table, n_rh, n_core, n_col, n_rows, n_cols):
     total = n_rh * n_core * n_rows
     n_pa = n_core * n_rows // n_col
     n_lt = total // n_core // LANES
     return pl.pallas_call(
         functools.partial(triangle_kernel, n_rh, n_core, n_col, n_rows, n_cols),
+        in_specs=[pl.BlockSpec(), pl.BlockSpec(memory_space=pl.ANY)],
         out_shape=jax.ShapeDtypeStruct((sides.shape[0], n_lt * n_pa, LANES), BF),
         scratch_shapes=[
             pltpu.VMEM((total, n_col * LANES), BF),
@@ -179,7 +180,7 @@
         ],
         compiler_params=pltpu.CompilerParams(vmem_limit_bytes=24 << 20),
         name="triangle",
-    )(sides)
+    )(sides, table)
 
 
 def unit_norm(x, ones):
@@ -536,13 +537,6 @@
     n_pa = n_core * sub
     n_q = n_col * half
 
-    packed = jnp.concatenate(
-        [coords, chain_ids.astype(F32)[None], coord_mask.astype(F32)[None]], axis=0
-    )
-    packed = jnp.broadcast_to(packed, (n_rh * n_core, *packed.shape))
-    known = exchange(packed, ("rh", "core"))
-    known = known.reshape(n_rh, n_core, -1, row_count)
-
     w_sides = w_tri_in[:, : 4 * ch].T
     sides, *pieces = make_sides(col.reshape(1), pair_in, gain_tri, w_sides, n_col)
     sides = exchange(sides, every)
@@ -556,13 +550,24 @@
     give = lax.dynamic_index_in_dim(whole, 1 - core, 2, keepdims=False)
     other_pair = lax.ppermute(give, "core", [(0, 1), (1, 0)])
 
+    table = jnp.concatenate(
+        [coords, chain_ids.astype(F32)[None], coord_mask.astype(F32)[None]], axis=0
+    ).reshape(1, -1)
+    n_row = n_rh * n_core
+    for step in (1, 4):
+        swaps = [[(r, r ^ (step * d)) for r in range(n_row)] for d in range(1, 4)]
+        table = jnp.concatenate(
+            [table] + [lax.ppermute(table, ("rh", "core"), swap) for swap in swaps], axis=0
+        )
+    at = jnp.arange(n_row) ^ (rh * n_core + core)
+    known = table[at].reshape(n_rh, n_core, -1, row_count)
     near = lax.dynamic_index_in_dim(known, rh, 0, keepdims=False)
     near = near.transpose(1, 0, 2).reshape(-1, n_core, sub, n_col)
     near = lax.dynamic_index_in_dim(near, col, 3, keepdims=False).reshape(-1, n_pa)
     far = lax.dynamic_index_in_dim(known, core, 1, keepdims=False)
     far = far.transpose(1, 0, 2).reshape(-1, n_q)
 
-    product = triangle(sides, n_rh, n_core, n_col, row_count, col_count)
+    product = triangle(sides, table, n_rh, n_core, n_col, row_count, col_count)
     back = exchange(product, every)
     two, normed, bias = update(
         (n_rh, n_core, n_col),

time: 212 us -> 213 us (level)
  starting transfers between devices: 47.9 us -> 51.7 us
  waiting for transfers between devices: 51.4 us -> 47.8 us
    ppermute x7, waiting for transfers between devices: 20.9 us -> 0.02 us  [body(): lax.ppermute(pieces[d], 'col', [(i, (i + d) % n_col) for i in range(n_col)])]
    ppermute x0 -> x6, waiting for transfers between devices: none -> 17.2 us  [body(): lax.ppermute(table, ('rh', 'core'), swap)]
    ppermute x0 -> x6, starting transfers between devices: none -> 7.97 us  [body(): lax.ppermute(table, ('rh', 'core'), swap)]
    all_to_all x4 -> x3, starting transfers between devices: 28.9 us -> 23.4 us  [exchange(): return lax.all_to_all(x, axes, split_axis=0, concat_axis=0, tiled=True)]
    unnamed x36 -> x42, local copies, waits for them, and re-layouts: 15.4 us -> 13.9 us
    all_to_all x4 -> x3, waiting for transfers between devices: 30.5 us -> 30.7 us  [exchange(): return lax.all_to_all(x, axes, split_axis=0, concat_axis=0, tiled=True)]
  transfers between devices with their start and end apart: 13 -> 18, of which waited for: 4 -> 4; matrix products, arithmetic and copies ran while one was open for 10% -> 10% of each run, Pallas kernels for 4% -> 4%
where the time goes in v3:
time: 213 us; the launch traced here: 212 us
  Pallas kernels  59.4 us (28%)
  starting transfers between devices  51.7 us (24%)
  waiting for transfers between devices  47.8 us (22%)
  local copies, waits for them, and re-layouts  25.9 us (12%)
  blocking collectives  24.3 us (11%)
  other arithmetic  2.52 us (1%)
    pallas_call x1, Pallas kernels, attention(): pl.pallas_call(attention_kernel, grid=(2 * steps,), in_specs=[pl.BlockSpe...  33 us
    all_to_all x3, waiting for transfers between devices, exchange(): return lax.all_to_all(x, axes, split_axis=0, concat_axis=0, tiled=True)  30.7 us
    all_to_all x1, blocking collectives, exchange(): return lax.all_to_all(x, axes, split_axis=0, concat_axis=0, tiled=True)  24.3 us
    all_to_all x3, starting transfers between devices, exchange(): return lax.all_to_all(x, axes, split_axis=0, concat_axis=0, tiled=True)  23.4 us
    ppermute x7, starting transfers between devices, body(): lax.ppermute(pieces[d], 'col', [(i, (i + d) % n_col) for i in range(n_col)])  18 us
    ppermute x6, waiting for transfers between devices, body(): lax.ppermute(table, ('rh', 'core'), swap)  17.2 us
    unnamed x42, local copies, waits for them, and re-layouts  13.9 us
    pallas_call x1, Pallas kernels, update(): pl.pallas_call(functools.partial(update_kernel, n_bins), grid=(n_pa // n_...  9.1 us
  transfers between devices with their start and end apart: 18, of which 4 were waited for; matrix products, arithmetic and copies ran while one was open for 10% of the time, Pallas kernels for 4%

profile of v3, /device:TPU:1, one launch (start us, length us, event | category | flops | bytes accessed | tf_op | source)
XLA Modules:
  0.0 211.9 jit_solution(5313666884508632338)
XLA Ops:
  0.0 0.9 slice.15
  0.9 0.8 copy.59
  1.7 8.3 %sides.1 = (bf16[128,72,128]{2,1,0:T(8,128)(2,1)}, bf16[6,96,128]{2,1,0:T(8,128)(2,1)}, bf16[6,96,128]{2,1,0:T(8,128)(2,1)}, bf16[6,96,128]{2,1,0:T(8,128)(2,1)}...) custom-call(s32[1]{0:T(128)} %bitcast.1.col_ref, ...), custom_call_target="tpu_custom_call" | custom-call | tf_op jit(solution)/shard_map/sides/pallas_call | solution.py:105
  10.0 11.5 %all-to-all-start = ((bf16[128,72,128]{2,1,0:T(8,128)(2,1)}), bf16[128,72,128]{2,1,0:T(8,128)(2,1)S(1)}, u32[]{:S(2)}, u32[]{:S(2)}) async-start(bf16[128,72,128]{2,1,0:T(8,128)(2,1)} %get-tuple-element.21), calls=%async_computation | async-start | bytes 4718592 | tf_op jit(solution)/shard_map/all_to_all | solution.py:34
  21.5 0.1 reshape.77
  21.6 1.7 collective-permute-start.2
  23.3 0.8 collective-permute-start.1
  24.1 1.2 collective-permute-start.6
  25.3 2.9 %collective-permute-start.7 = (bf16[6,96,128]{2,1,0:T(8,128)(2,1)}, bf16[6,96,128]{2,1,0:T(8,128)(2,1)}, u32[]{:S(2)}, u32[]{:S(2)}) collective-permute-start(bf16[6,96,128]{2,1,0:T(8,128)(2,1)} %get-tuple-element.24), channel_id=1, source_target_pairs={{0,2},{1,3},{2,4},{3,5},{4,6},{5,7},{6,0},{7,1},{8,10},{9,11},{10,... | collective-permute-start | bytes 442376 | tf_op jit(solution)/shard_map/ppermute | solution.py:545
  28.2 0.9 constant_dynamic-update-slice_fusion.7
  29.2 17.0 %collective-permute-done.2 = f32[1,240]{1,0:T(1,128)S(1)} collective-permute-done((f32[1,240]{1,0:T(1,128)S(1)}, f32[1,240]{1,0:T(1,128)S(1)}, u32[]{:S(2)}, u32[]{:S(2)}) %collective-permute-start.2) | collective-permute-done | bytes 992 | tf_op jit(solution)/shard_map/ppermute | solution.py:560
  46.2 0.7 pad_maximum_fusion.2
  46.9 4.8 %collective-permute-start.5 = (f32[4,240]{1,0:T(4,128)S(1)}, f32[4,240]{1,0:T(4,128)}, u32[]{:S(2)}, u32[]{:S(2)}) collective-permute-start(f32[4,240]{1,0:T(4,128)S(1)} %pad_maximum_fusion.2), channel_id=1, source_target_pairs={{0,96},{8,104},{16,112},{24,120},{32,64},{40,72},{48,80},{56,88},{... | collective-permute-start | bytes 11528 | tf_op jit(solution)/shard_map/ppermute | solution.py:560
  51.7 0.4 collective-permute-start.4
  52.1 0.3 collective-permute-start.3
  52.4 0.6 fusion.1
  53.0 0.1 collective-permute-done.5
  53.1 4.1 %collective-permute-start.8 = (bf16[6,96,128]{2,1,0:T(8,128)(2,1)}, bf16[6,96,128]{2,1,0:T(8,128)(2,1)}, u32[]{:S(2)}, u32[]{:S(2)}) collective-permute-start(bf16[6,96,128]{2,1,0:T(8,128)(2,1)} %get-tuple-element.25), channel_id=1, source_target_pairs={{0,3},{1,4},{2,5},{3,6},{4,7},{5,0},{6,1},{7,2},{8,11},{9,12},{10,... | collective-permute-start | bytes 442376 | tf_op jit(solution)/shard_map/ppermute | solution.py:545
  57.2 2.1 collective-permute-start.9
  59.3 0.1 collective-permute-start.10
  59.3 1.5 concatenate.20.table_ref
  60.8 6.4 %collective-permute-start.11 = (bf16[6,96,128]{2,1,0:T(8,128)(2,1)}, bf16[6,96,128]{2,1,0:T(8,128)(2,1)}, u32[]{:S(2)}, u32[]{:S(2)}) collective-permute-start(bf16[6,96,128]{2,1,0:T(8,128)(2,1)} %get-tuple-element.28), channel_id=1, source_target_pairs={{0,6},{1,7},{2,0},{3,1},{4,2},{5,3},{6,4},{7,5},{8,14},{9,15},{10,... | collective-permute-start | bytes 442376 | tf_op jit(solution)/shard_map/ppermute | solution.py:545
  67.2 0.9 constant_dynamic-update-slice_fusion.6
  68.2 1.2 collective-permute-start.12
  69.4 0.9 constant_dynamic-update-slice_fusion.5
  70.3 0.9 constant_dynamic-update-slice_fusion.4
  71.3 3.3 %triangle.1 = bf16[128,36,128]{2,1,0:T(8,128)(2,1)S(1)} custom-call(bf16[128,72,128]{2,1,0:T(8,128)(2,1)S(1)} %all-to-all-done.in_ref, f32[16,240]{1,0:T(8,128)S(1)} %concatenate.20.table_ref), custom_call_target="tpu_custom_call" | custom-call | tf_op jit(solution)/shard_map/triangle/pallas_call | solution.py:172
  74.6 1.1 copy-done
  75.7 6.7 %all-to-all-start.1 = ((bf16[128,36,128]{2,1,0:T(8,128)(2,1)}), bf16[128,36,128]{2,1,0:T(8,128)(2,1)S(1)}, u32[]{:S(2)}, u32[]{:S(2)}) async-start(bf16[128,36,128]{2,1,0:T(8,128)(2,1)} %copy-done), calls=%async_computation.1 | async-start | bytes 2621440 | tf_op jit(solution)/shard_map/all_to_all | solution.py:34
  82.4 0.9 constant_dynamic-update-slice_fusion.3
  83.3 0.9 constant_dynamic-update-slice_fusion.2
  84.2 0.9 constant_dynamic-update-slice_fusion.1
  85.2 0.9 constant_dynamic-update-slice_fusion
  86.1 0.0 copy-start.11
  86.1 0.0 copy-start.10
  86.2 0.0 copy-start.5
  86.2 0.0 copy-start.12
  86.2 1.1 dynamic-slice_bitcast_fusion
  87.3 1.1 collective-permute-start.13
  88.3 0.6 pad_add_fusion.place_ref
  88.9 1.4 slice.16.wgo_ref
  90.3 0.7 copy.54.gain_sum_ref
  91.1 0.6 pad.9.wbias_ref
  91.7 0.6 pad_maximum_fusion.wbins_ref
  92.3 0.6 gather_fusion
  92.9 0.1 reshape.78
  93.0 0.7 reshape.81.far_ref
  93.7 0.1 reshape.79
  93.8 0.2 dynamic-slice_reduce_fusion
  93.9 0.7 reshape.80.near_ref
  94.6 9.3 %all-to-all-done.1.back_ref = bf16[128,36,128]{2,1,0:T(8,128)(2,1)S(1)} async-done(((bf16[128,36,128]{2,1,0:T(8,128)(2,1)}), bf16[128,36,128]{2,1,0:T(8,128)(2,1)S(1)}, u32[]{:S(2)}, u32[]{:S(2)}) %all-to-all-start.1) | async-done | bytes 1179680 | tf_op jit(solution)/shard_map/all_to_all | solution.py:34
  103.9 1.1 copy-done.2
  105.0 9.1 %update.1 = (bf16[12,384,128]{2,1,0:T(8,128)(2,1)}, bf16[12,384,128]{2,1,0:T(8,128)(2,1)}, bf16[8,2,8,24,384]{4,3,2,1,0:T(8,128)(2,1)}) custom-call(s32[2]{0:T(128)} %pad_add_fusion.place_ref, bf16[128,36,128]{2,1,0:T(8,128)(2,1)} %copy-done.2, bf16[8,6,48,128]{3,2,1,0:T(8,128)(2,1)} %get-tuple-element.38.keep_ref, bf16[8,6,48,128]{3,2,1,0:T(8,128)(2,1)} %copy-done.4, ...), custom_call_target="tpu_custom_call" | custom-call | tf_op jit(solution)/shard_map/update/pallas_call | solution.py:302
  114.1 5.3 %all-to-all-start.2 = ((bf16[128,24,384]{2,1,0:T(8,128)(2,1)}), bf16[128,24,384]{2,1,0:T(8,128)(2,1)S(1)}, u32[]{:S(2)}, u32[]{:S(2)}) async-start(bf16[128,24,384]{2,1,0:T(8,128)(2,1)} %bitcast.50), calls=%async_computation.2 | async-start | bytes 4718592 | tf_op jit(solution)/shard_map/all_to_all | solution.py:34
  119.4 1.3 collective-permute-start.14
  120.6 1.4 fusion.2
  122.1 1.5 copy.63
  123.5 1.5 copy.62
  125.0 5.7 %project.1 = (bf16[12,384,128]{2,1,0:T(8,128)(2,1)}, bf16[12,768,128]{2,1,0:T(8,128)(2,1)}, bf16[12,4,48,768]{3,2,1,0:T(8,128)(2,1)}, f32[12,128,384]{2,1,0:T(8,128)}) custom-call(s32[1]{0:T(128)} %bitcast.core_ref, bf16[12,384,128]{2,1,0:T(8,128)(2,1)} %get-tuple-element.30.own_ref, bf16[12,384,128]{2,1,0:T(8,128)(2,1)} %collective-permute-done.14.other_ref, ...), custom_call_target="tpu_custom_call" | custom-call | tf_op jit(solution)/shard_map/project/pallas_call | solution.py:366
  130.7 21.4 %all-to-all-done.2.bias_ref = bf16[128,24,384]{2,1,0:T(8,128)(2,1)S(1)} async-done(((bf16[128,24,384]{2,1,0:T(8,128)(2,1)}), bf16[128,24,384]{2,1,0:T(8,128)(2,1)S(1)}, u32[]{:S(2)}, u32[]{:S(2)}) %all-to-all-start.2) | async-done | bytes 2359328 | tf_op jit(solution)/shard_map/all_to_all | solution.py:34
  152.1 1.4 copy-done.1
  153.5 33.0 %attention.1 = bf16[2,8,6,48,128]{4,3,2,1,0:T(8,128)(2,1)} custom-call(bf16[12,384,128]{2,1,0:T(8,128)(2,1)} %get-tuple-element.31.q_ref, bf16[12,768,128]{2,1,0:T(8,128)(2,1)} %get-tuple-element.32.k_ref, bf16[12,4,48,768]{3,2,1,0:T(8,128)(2,1)} %get-tuple-element.33.vt_ref, f32[12,128,384]{2,1,0:T(8,128)} %get-tuple-element.34.gate_ref, ...), custom_call_target="tpu_custom_call" | custom-call | tf_op jit(solution)/shard_map/attention/pallas_call | solution.py:487
  186.5 24.3 %all_to_all.20 = bf16[16,6,48,128]{3,2,1,0:T(8,128)(2,1)S(1)} all-to-all(bf16[16,6,48,128]{3,2,1,0:T(8,128)(2,1)} %bitcast.48), channel_id=1, replica_groups=mesh['rh'=8,'core'=2,'col'=8] {'core','col'}, dimensions={0} | all-to-all | bytes 2359296 | tf_op jit(solution)/shard_map/all_to_all | solution.py:34
  210.8 1.1 copy.57
  (48 shorter events, 0.1 us)
Async XLA Ops:
  10.0 11.5 %copy-start.14 = (s32[48]{0:T(128)S(1)}, s32[48]{0:T(128)}, u32[]{:S(2)}) copy-start(s32[48]{0:T(128)} %param.18) | copy-start | bytes 580
  10.0 11.5 %copy-start.15 = (s32[48]{0:T(128)S(1)}, s32[48]{0:T(128)}, u32[]{:S(2)}) copy-start(s32[48]{0:T(128)} %param.17) | copy-start | bytes 580
  10.0 11.5 %copy-start.9 = (f32[3,48]{1,0:T(4,128)S(1)}, f32[3,48]{1,0:T(4,128)}, u32[]{:S(2)}) copy-start(f32[3,48]{1,0:T(4,128)} %param.16) | copy-start | bytes 1732
  10.0 61.3 %all-to-all-start = ((bf16[128,72,128]{2,1,0:T(8,128)(2,1)}), bf16[128,72,128]{2,1,0:T(8,128)(2,1)S(1)}, u32[]{:S(2)}, u32[]{:S(2)}) async-start(bf16[128,72,128]{2,1,0:T(8,128)(2,1)} %get-tuple-element.21), calls=%async_computation | async-start | bytes 4718592 | tf_op jit(solution)/shard_map/all_to_all | solution.py:34
  21.6 37.6 %copy-start.6 = (f32[1,240]{1,0:T(1,128)}, f32[1,240]{1,0:T(1,128)S(1)}, u32[]{:S(2)}) copy-start(f32[1,240]{1,0:T(1,128)S(1)} %reshape.77) | copy-start | bytes 2884
  21.6 24.5 %collective-permute-start.2 = (f32[1,240]{1,0:T(1,128)S(1)}, f32[1,240]{1,0:T(1,128)S(1)}, u32[]{:S(2)}, u32[]{:S(2)}) collective-permute-start(f32[1,240]{1,0:T(1,128)S(1)} %reshape.77), channel_id=1, source_target_pairs={{0,24},{8,16},{16,8},{24,0},{32,56},{40,48},{48,40},{56,32},{64,88... | collective-permute-start | bytes 2888 | tf_op jit(solution)/shard_map/ppermute | solution.py:560
  23.3 22.9 %collective-permute-start.1 = (f32[1,240]{1,0:T(1,128)S(1)}, f32[1,240]{1,0:T(1,128)S(1)}, u32[]{:S(2)}, u32[]{:S(2)}) collective-permute-start(f32[1,240]{1,0:T(1,128)S(1)} %reshape.77), channel_id=1, source_target_pairs={{0,16},{8,24},{16,0},{24,8},{32,48},{40,56},{48,32},{56,40},{64,80... | collective-permute-start | bytes 2888 | tf_op jit(solution)/shard_map/ppermute | solution.py:560
  24.1 22.1 %collective-permute-start = (f32[1,240]{1,0:T(1,128)S(1)}, f32[1,240]{1,0:T(1,128)}, u32[]{:S(2)}, u32[]{:S(2)}) collective-permute-start(f32[1,240]{1,0:T(1,128)S(1)} %reshape.77), channel_id=1, source_target_pairs={{0,8},{8,0},{16,24},{24,16},{32,40},{40,32},{48,56},{56,48},{64,72... | collective-permute-start | bytes 2888 | tf_op jit(solution)/shard_map/ppermute | solution.py:560
  24.1 36.7 %collective-permute-start.6 = (bf16[6,96,128]{2,1,0:T(8,128)(2,1)}, bf16[6,96,128]{2,1,0:T(8,128)(2,1)}, u32[]{:S(2)}, u32[]{:S(2)}) collective-permute-start(bf16[6,96,128]{2,1,0:T(8,128)(2,1)} %get-tuple-element.23), channel_id=1, source_target_pairs={{0,1},{1,2},{2,3},{3,4},{4,5},{5,6},{6,7},{7,0},{8,9},{9,10},{10,1... | collective-permute-start | bytes 442376 | tf_op jit(solution)/shard_map/ppermute | solution.py:545
  25.3 42.9 %collective-permute-start.7 = (bf16[6,96,128]{2,1,0:T(8,128)(2,1)}, bf16[6,96,128]{2,1,0:T(8,128)(2,1)}, u32[]{:S(2)}, u32[]{:S(2)}) collective-permute-start(bf16[6,96,128]{2,1,0:T(8,128)(2,1)} %get-tuple-element.24), channel_id=1, source_target_pairs={{0,2},{1,3},{2,4},{3,5},{4,6},{5,7},{6,0},{7,1},{8,10},{9,11},{10,... | collective-permute-start | bytes 442376 | tf_op jit(solution)/shard_map/ppermute | solution.py:545
  46.2 13.1 %copy-start.7 = (f32[1,240]{1,0:T(1,128)}, f32[1,240]{1,0:T(1,128)S(1)}, u32[]{:S(2)}) copy-start(f32[1,240]{1,0:T(1,128)S(1)} %collective-permute-done.2) | copy-start | bytes 2884
  46.2 13.1 %copy-start.8 = (f32[1,240]{1,0:T(1,128)}, f32[1,240]{1,0:T(1,128)S(1)}, u32[]{:S(2)}) copy-start(f32[1,240]{1,0:T(1,128)S(1)} %collective-permute-done.1) | copy-start | bytes 2884
  46.9 6.2 %collective-permute-start.5 = (f32[4,240]{1,0:T(4,128)S(1)}, f32[4,240]{1,0:T(4,128)}, u32[]{:S(2)}, u32[]{:S(2)}) collective-permute-start(f32[4,240]{1,0:T(4,128)S(1)} %pad_maximum_fusion.2), channel_id=1, source_target_pairs={{0,96},{8,104},{16,112},{24,120},{32,64},{40,72},{48,80},{56,88},{... | collective-permute-start | bytes 11528 | tf_op jit(solution)/shard_map/ppermute | solution.py:560
  51.7 5.5 %collective-permute-start.4 = (f32[4,240]{1,0:T(4,128)S(1)}, f32[4,240]{1,0:T(4,128)}, u32[]{:S(2)}, u32[]{:S(2)}) collective-permute-start(f32[4,240]{1,0:T(4,128)S(1)} %pad_maximum_fusion.2), channel_id=1, source_target_pairs={{0,64},{8,72},{16,80},{24,88},{32,96},{40,104},{48,112},{56,120},{... | collective-permute-start | bytes 11528 | tf_op jit(solution)/shard_map/ppermute | solution.py:560
  52.1 7.1 %collective-permute-start.3 = (f32[4,240]{1,0:T(4,128)S(1)}, f32[4,240]{1,0:T(4,128)}, u32[]{:S(2)}, u32[]{:S(2)}) collective-permute-start(f32[4,240]{1,0:T(4,128)S(1)} %pad_maximum_fusion.2), channel_id=1, source_target_pairs={{0,32},{8,40},{16,48},{24,56},{32,0},{40,8},{48,16},{56,24},{64,96... | collective-permute-start | bytes 11528 | tf_op jit(solution)/shard_map/ppermute | solution.py:560
  53.1 17.2 %collective-permute-start.8 = (bf16[6,96,128]{2,1,0:T(8,128)(2,1)}, bf16[6,96,128]{2,1,0:T(8,128)(2,1)}, u32[]{:S(2)}, u32[]{:S(2)}) collective-permute-start(bf16[6,96,128]{2,1,0:T(8,128)(2,1)} %get-tuple-element.25), channel_id=1, source_target_pairs={{0,3},{1,4},{2,5},{3,6},{4,7},{5,0},{6,1},{7,2},{8,11},{9,12},{10,... | collective-permute-start | bytes 442376 | tf_op jit(solution)/shard_map/ppermute | solution.py:545
  57.2 25.2 %collective-permute-start.9 = (bf16[6,96,128]{2,1,0:T(8,128)(2,1)}, bf16[6,96,128]{2,1,0:T(8,128)(2,1)}, u32[]{:S(2)}, u32[]{:S(2)}) collective-permute-start(bf16[6,96,128]{2,1,0:T(8,128)(2,1)} %get-tuple-element.26), channel_id=1, source_target_pairs={{0,4},{1,5},{2,6},{3,7},{4,0},{5,1},{6,2},{7,3},{8,12},{9,13},{10,... | collective-permute-start | bytes 442376 | tf_op jit(solution)/shard_map/ppermute | solution.py:545
  59.3 24.0 %collective-permute-start.10 = (bf16[6,96,128]{2,1,0:T(8,128)(2,1)}, bf16[6,96,128]{2,1,0:T(8,128)(2,1)}, u32[]{:S(2)}, u32[]{:S(2)}) collective-permute-start(bf16[6,96,128]{2,1,0:T(8,128)(2,1)} %get-tuple-element.27), channel_id=1, source_target_pairs={{0,5},{1,6},{2,7},{3,0},{4,1},{5,2},{6,3},{7,4},{8,13},{9,14},{10,... | collective-permute-start | bytes 442376 | tf_op jit(solution)/shard_map/ppermute | solution.py:545
  60.8 23.4 %collective-permute-start.11 = (bf16[6,96,128]{2,1,0:T(8,128)(2,1)}, bf16[6,96,128]{2,1,0:T(8,128)(2,1)}, u32[]{:S(2)}, u32[]{:S(2)}) collective-permute-start(bf16[6,96,128]{2,1,0:T(8,128)(2,1)} %get-tuple-element.28), channel_id=1, source_target_pairs={{0,6},{1,7},{2,0},{3,1},{4,2},{5,3},{6,4},{7,5},{8,14},{9,15},{10,... | collective-permute-start | bytes 442376 | tf_op jit(solution)/shard_map/ppermute | solution.py:545
  68.2 17.0 %collective-permute-start.12 = (bf16[6,96,128]{2,1,0:T(8,128)(2,1)}, bf16[6,96,128]{2,1,0:T(8,128)(2,1)}, u32[]{:S(2)}, u32[]{:S(2)}) collective-permute-start(bf16[6,96,128]{2,1,0:T(8,128)(2,1)} %get-tuple-element.29), channel_id=1, source_target_pairs={{0,7},{1,0},{2,1},{3,2},{4,3},{5,4},{6,5},{7,6},{8,15},{9,8},{10,9... | collective-permute-start | bytes 442376 | tf_op jit(solution)/shard_map/ppermute | solution.py:545
  74.6 1.1 copy-start
  75.7 28.2 %all-to-all-start.1 = ((bf16[128,36,128]{2,1,0:T(8,128)(2,1)}), bf16[128,36,128]{2,1,0:T(8,128)(2,1)S(1)}, u32[]{:S(2)}, u32[]{:S(2)}) async-start(bf16[128,36,128]{2,1,0:T(8,128)(2,1)} %copy-done), calls=%async_computation.1 | async-start | bytes 2621440 | tf_op jit(solution)/shard_map/all_to_all | solution.py:34
  86.1 4.2 %copy-start.11 = (f32[128]{0:T(128)S(1)}, f32[128]{0:T(128)}, u32[]{:S(2)}) copy-start(f32[128]{0:T(128)} %param.20) | copy-start | bytes 1540
  86.1 4.9 %copy-start.10 = (bf16[128,4]{0,1:T(4,128)(2,1)S(1)}, bf16[128,4]{0,1:T(4,128)(2,1)}, u32[]{:S(2)}) copy-start(bf16[128,4]{0,1:T(4,128)(2,1)} %param.28) | copy-start | bytes 3076
  86.1 5.5 %copy-start.13 = (s32[16]{0:T(128)S(1)}, s32[16]{0:T(128)}, u32[]{:S(2)}) copy-start(s32[16]{0:T(128)} %fusion.1) | copy-start | bytes 196
  86.2 5.5 %copy-start.5 = (f32[36,128]{1,0:T(8,128)S(1)}, f32[36,128]{1,0:T(8,128)}, u32[]{:S(2)}) copy-start(f32[36,128]{1,0:T(8,128)} %param.24) | copy-start | bytes 55300
  86.2 5.5 %copy-start.12 = (f32[128]{0:T(128)S(1)}, f32[128]{0:T(128)}, u32[]{:S(2)}) copy-start(f32[128]{0:T(128)} %param.25) | copy-start | bytes 1540
  87.3 7.3 %collective-permute-start.13 = (bf16[8,6,48,128]{3,2,1,0:T(8,128)(2,1)}, bf16[8,6,48,128]{3,2,1,0:T(8,128)(2,1)S(1)}, u32[]{:S(2)}, u32[]{:S(2)}) collective-permute-start(bf16[8,6,48,128]{3,2,1,0:T(8,128)(2,1)} %get-tuple-element.37), channel_id=1, source_target_pairs={{0,8},{8,0},{1,9},{9,1},{2,10},{10,2},{3,11},{11,3},{4,12},{12,4},... | collective-permute-start | bytes 1769480 | tf_op jit(solution)/shard_map/ppermute | solution.py:551
  94.6 9.3 %copy-start.4 = (bf16[8,6,48,128]{3,2,1,0:T(8,128)(2,1)}, bf16[8,6,48,128]{3,2,1,0:T(8,128)(2,1)S(1)}, u32[]{:S(2)}) copy-start(bf16[8,6,48,128]{3,2,1,0:T(8,128)(2,1)S(1)} %collective-permute-done.13.other_ref) | copy-start | bytes 1769476
  103.9 1.1 copy-start.2
  114.1 5.3 %copy-start.3 = (bf16[12,384,128]{2,1,0:T(8,128)(2,1)S(1)}, bf16[12,384,128]{2,1,0:T(8,128)(2,1)}, u32[]{:S(2)}) copy-start(bf16[12,384,128]{2,1,0:T(8,128)(2,1)} %get-tuple-element.30.own_ref) | copy-start | bytes 3538948
  114.1 38.0 %all-to-all-start.2 = ((bf16[128,24,384]{2,1,0:T(8,128)(2,1)}), bf16[128,24,384]{2,1,0:T(8,128)(2,1)S(1)}, u32[]{:S(2)}, u32[]{:S(2)}) async-start(bf16[128,24,384]{2,1,0:T(8,128)(2,1)} %bitcast.50), calls=%async_computation.2 | async-start | bytes 4718592 | tf_op jit(solution)/shard_map/all_to_all | solution.py:34
  119.4 5.7 %collective-permute-start.14 = (bf16[12,384,128]{2,1,0:T(8,128)(2,1)S(1)}, bf16[12,384,128]{2,1,0:T(8,128)(2,1)}, u32[]{:S(2)}, u32[]{:S(2)}) collective-permute-start(bf16[12,384,128]{2,1,0:T(8,128)(2,1)S(1)} %copy-done.3), channel_id=1, source_target_pairs={{0,8},{1,9},{2,10},{3,11},{4,12},{5,13},{6,14},{7,15},{8,0},{9,1},... | collective-permute-start | bytes 3538952 | tf_op jit(solution)/shard_map/ppermute | solution.py:590
  152.1 1.4 copy-start.1

commit v4 on v3

--- a/solution.py
+++ b/solution.py
@@ -35,9 +35,10 @@
 
 
 def sides_kernel(col_ref, x_ref, gain_ref, w_ref, out_ref, *rest_refs):
-    piece_refs, norm_sc, sc = rest_refs[:-2], rest_refs[-2], rest_refs[-1]
+    piece_refs, (norm_sc, sc, w_sc) = rest_refs[:-3], rest_refs[-3:]
     n_rows, n_cols, ch = x_ref.shape
     n_col = len(piece_refs)
+    w_sc[...] = w_ref[:, : 4 * ch].astype(F32).T.astype(BF)
     for shift, piece_ref in enumerate(piece_refs):
         for a in range(n_rows // n_col):
             piece_ref[a] = x_ref[a * n_col + (col_ref[0] + shift) % n_col]
@@ -53,7 +54,7 @@
     lax.fori_loop(0, n_rows // 4, norm, 0, unroll=2)
 
     def sides(x):
-        pr = dot_nt(w_ref[...], x)
+        pr = dot_nt(w_sc[...], x)
         left = jax.nn.sigmoid(pr[:ch]) * pr[ch : 2 * ch]
         right = jax.nn.sigmoid(pr[2 * ch : 3 * ch]) * pr[3 * ch :]
         return left, right
@@ -98,7 +99,7 @@
     lax.fori_loop(0, ch, emit, 0, unroll=16)
 
 
-def make_sides(col, pair, gain, w_t, n_col):
+def make_sides(col, pair, gain, w, n_col):
     n_rows, n_cols, ch = pair.shape
     n_out = 2 * n_rows * n_cols // LANES
     piece = jax.ShapeDtypeStruct((n_rows // n_col, n_cols, ch), BF)
@@ -109,9 +110,10 @@
         scratch_shapes=[
             pltpu.VMEM(pair.shape, BF),
             pltpu.VMEM((ch * n_out, LANES), F32),
+            pltpu.VMEM((4 * ch, ch), BF),
         ],
         name="sides",
-    )(col, pair, gain.reshape(1, ch), w_t)
+    )(col, pair, gain.reshape(1, ch), w)
 
 
 def triangle_kernel(n_rh, n_core, n_col, n_rows, n_cols, in_ref, table_ref, out_ref, l_sc, r_sc, p_sc):
@@ -181,6 +183,28 @@
         compiler_params=pltpu.CompilerParams(vmem_limit_bytes=24 << 20),
         name="triangle",
     )(sides, table)
+
+
+def split_kernel(core_ref, *refs):
+    pieces, (keep_ref, give_ref) = refs[:-3], refs[-2:]
+    half = keep_ref.shape[2]
+    core = core_ref[0]
+    for s, piece in enumerate(pieces):
+        keep_ref[s] = piece[:, pl.ds(pl.multiple_of(core * half, 16), half), :]
+        give_ref[s] = piece[:, pl.ds(pl.multiple_of((1 - core) * half, 16), half), :]
+
+
+def split(core, pieces, product):
+    sub, n_cols, ch = pieces[0].shape
+    out = jax.ShapeDtypeStruct((len(pieces), sub, n_cols // 2, ch), BF)
+    return pl.pallas_call(
+        split_kernel,
+        in_specs=[pl.BlockSpec(memory_space=pltpu.SMEM)]
+        + [pl.BlockSpec()] * len(pieces)
+        + [pl.BlockSpec(memory_space=pl.ANY)],
+        out_shape=[out, out],
+        name="split",
+    )(core, *pieces, product)
 
 
 def unit_norm(x, ones):
@@ -330,6 +354,7 @@
             jax.ShapeDtypeStruct((n_rh, n_core, n_col, sub * n_heads, n_q), BF),
         ],
         scratch_shapes=[pltpu.VMEM((ch * n_in8, LANES), F32)],
+        compiler_params=pltpu.CompilerParams(vmem_limit_bytes=44 << 20),
         name="update",
     )(place, back, keep, other, near, far, gains[0], gains[1], gains[2], wgo, wout, wbins, wbias_t)
 
@@ -473,7 +498,7 @@
             s = ahead
         return carry
 
-    lax.fori_loop(0, q_ref.shape[0], row, 0)
+    lax.fori_loop(0, q_ref.shape[0], row, 0, unroll=3)
 
 
 def attention(q, k, vt, gate, two, bias, wo, n_col, n_row=3):
@@ -537,19 +562,13 @@
     n_pa = n_core * sub
     n_q = n_col * half
 
-    w_sides = w_tri_in[:, : 4 * ch].T
-    sides, *pieces = make_sides(col.reshape(1), pair_in, gain_tri, w_sides, n_col)
+    sides, *pieces = make_sides(col.reshape(1), pair_in, gain_tri, w_tri_in, n_col)
     sides = exchange(sides, every)
 
     pieces = [pieces[0]] + [
         lax.ppermute(pieces[d], "col", [(i, (i + d) % n_col) for i in range(n_col)])
         for d in range(1, n_col)
     ]
-    whole = jnp.stack(pieces).reshape(n_col, sub, n_core, half, ch)
-    keep = lax.dynamic_index_in_dim(whole, core, 2, keepdims=False)
-    give = lax.dynamic_index_in_dim(whole, 1 - core, 2, keepdims=False)
-    other_pair = lax.ppermute(give, "core", [(0, 1), (1, 0)])
-
     table = jnp.concatenate(
         [coords, chain_ids.astype(F32)[None], coord_mask.astype(F32)[None]], axis=0
     ).reshape(1, -1)
@@ -568,6 +587,8 @@
     far = far.transpose(1, 0, 2).reshape(-1, n_q)
 
     product = triangle(sides, table, n_rh, n_core, n_col, row_count, col_count)
+    keep, give = split(core.reshape(1), pieces, product)
+    other_pair = lax.ppermute(give, "core", [(0, 1), (1, 0)])
     back = exchange(product, every)
     two, normed, bias = update(
         (n_rh, n_core, n_col),

time: 213 us -> 218 us (1.023)
  waiting for transfers between devices: 47.8 us -> 68.6 us
  local copies, waits for them, and re-layouts: 25.9 us -> 10.5 us
  starting transfers between devices: 51.7 us -> 54.6 us
  other arithmetic: 2.52 us -> 0.13 us
    ppermute x7, waiting for transfers between devices: 0.02 us -> 20.5 us  [body(): lax.ppermute(pieces[d], 'col', [(i, (i + d) % n_col) for i in range(n_col)])]
    all_to_all x3, waiting for transfers between devices: 30.7 us -> 21.9 us  [exchange(): return lax.all_to_all(x, axes, split_axis=0, concat_axis=0, tiled=True)]
    ppermute x6, waiting for transfers between devices: 17.2 us -> 25.7 us  [body(): lax.ppermute(table, ('rh', 'core'), swap)]
    unnamed x42 -> x62, local copies, waits for them, and re-layouts: 13.9 us -> 6.72 us
    all_to_all x3, starting transfers between devices: 23.4 us -> 30.2 us  [exchange(): return lax.all_to_all(x, axes, split_axis=0, concat_axis=0, tiled=True)]
    ppermute x7, starting transfers between devices: 18 us -> 14.6 us  [body(): lax.ppermute(pieces[d], 'col', [(i, (i + d) % n_col) for i in range(n_col)])]
    pallas_call x0 -> x1, Pallas kernels: none -> 2.48 us  [split(): pl.pallas_call(split_kernel, in_specs=[pl.BlockSpec(memory_space=pltpu.SM...]
  transfers between devices with their start and end apart: 18 -> 18, of which waited for: 4 -> 8; matrix products, arithmetic and copies ran while one was open for 10% -> 2% of each run, Pallas kernels for 4% -> 4%
where the time goes in v4:
time: 218 us; the launch traced here: 217 us
  waiting for transfers between devices  68.6 us (31%)
  Pallas kernels  59 us (27%)
  starting transfers between devices  54.6 us (25%)
  blocking collectives  24.3 us (11%)
  local copies, waits for them, and re-layouts  10.5 us (5%)
    pallas_call x1, Pallas kernels, attention(): pl.pallas_call(attention_kernel, grid=(2 * steps,), in_specs=[pl.BlockSpe...  31 us
    all_to_all x3, starting transfers between devices, exchange(): return lax.all_to_all(x, axes, split_axis=0, concat_axis=0, tiled=True)  30.2 us
    ppermute x6, waiting for transfers between devices, body(): lax.ppermute(table, ('rh', 'core'), swap)  25.7 us
    all_to_all x1, blocking collectives, exchange(): return lax.all_to_all(x, axes, split_axis=0, concat_axis=0, tiled=True)  24.3 us
    all_to_all x3, waiting for transfers between devices, exchange(): return lax.all_to_all(x, axes, split_axis=0, concat_axis=0, tiled=True)  21.9 us
    ppermute x7, waiting for transfers between devices, body(): lax.ppermute(pieces[d], 'col', [(i, (i + d) % n_col) for i in range(n_col)])  20.5 us
    ppermute x7, starting transfers between devices, body(): lax.ppermute(pieces[d], 'col', [(i, (i + d) % n_col) for i in range(n_col)])  14.6 us
    pallas_call x1, Pallas kernels, make_sides(): pl.pallas_call(sides_kernel, in_specs=[pl.BlockSpec(memory_space=pltpu.SM...  8.4 us
  transfers between devices with their start and end apart: 18, of which 8 were waited for; matrix products, arithmetic and copies ran while one was open for 2% of the time, Pallas kernels for 4%

profile of v4, /device:TPU:1, one launch (start us, length us, event | category | flops | bytes accessed | tf_op | source)
XLA Modules:
  0.0 217.4 jit_solution(3059255547956215408)
XLA Ops:
  0.0 8.4 %sides.1 = (bf16[128,72,128]{2,1,0:T(8,128)(2,1)}, bf16[6,96,128]{2,1,0:T(8,128)(2,1)}, bf16[6,96,128]{2,1,0:T(8,128)(2,1)}, bf16[6,96,128]{2,1,0:T(8,128)(2,1)}...) custom-call(s32[1]{0:T(128)} %bitcast.1.col_ref, ...), custom_call_target="tpu_custom_call" | custom-call | tf_op jit(solution)/shard_map/sides/pallas_call | solution.py:106
  8.4 11.5 %all-to-all-start = ((bf16[128,72,128]{2,1,0:T(8,128)(2,1)}), bf16[128,72,128]{2,1,0:T(8,128)(2,1)S(1)}, u32[]{:S(2)}, u32[]{:S(2)}) async-start(bf16[128,72,128]{2,1,0:T(8,128)(2,1)} %get-tuple-element.23), calls=%async_computation | async-start | bytes 4718592 | tf_op jit(solution)/shard_map/all_to_all | solution.py:34
  20.0 0.1 reshape.61
  20.1 1.7 collective-permute-start.2
  21.7 0.8 collective-permute-start.1
  22.5 0.0 collective-permute-start
  22.5 22.1 %collective-permute-done.2 = f32[1,240]{1,0:T(1,128)S(1)} collective-permute-done((f32[1,240]{1,0:T(1,128)S(1)}, f32[1,240]{1,0:T(1,128)S(1)}, u32[]{:S(2)}, u32[]{:S(2)}) %collective-permute-start.2) | collective-permute-done | bytes 992 | tf_op jit(solution)/shard_map/ppermute | solution.py:579
  44.6 0.0 collective-permute-done.1
  44.6 0.0 collective-permute-done
  44.6 4.8 %collective-permute-start.5 = (f32[4,240]{1,0:T(4,128)S(1)}, f32[4,240]{1,0:T(4,128)S(1)}, u32[]{:S(2)}, u32[]{:S(2)}) collective-permute-start(f32[4,240]{1,0:T(4,128)S(1)} %pad_maximum_fusion.2), channel_id=1, source_target_pairs={{0,96},{8,104},{16,112},{24,120},{32,64},{40,72},{48,80},{56,88},{... | collective-permute-start | bytes 11528 | tf_op jit(solution)/shard_map/ppermute | solution.py:579
  49.5 0.4 collective-permute-start.4
  49.9 0.3 collective-permute-start.3
  50.2 0.6 collective-permute-done.5
  50.8 3.0 %collective-permute-done.4 = f32[4,240]{1,0:T(4,128)S(1)} collective-permute-done((f32[4,240]{1,0:T(4,128)S(1)}, f32[4,240]{1,0:T(4,128)S(1)}, u32[]{:S(2)}, u32[]{:S(2)}) %collective-permute-start.4) | collective-permute-done | bytes 3872 | tf_op jit(solution)/shard_map/ppermute | solution.py:579
  53.7 0.0 collective-permute-done.3
  53.8 0.0 all-to-all-done.in_ref
  53.8 4.4 %triangle.1.refs_8_ = bf16[128,36,128]{2,1,0:T(8,128)(2,1)} custom-call(bf16[128,72,128]{2,1,0:T(8,128)(2,1)S(1)} %all-to-all-done.in_ref, f32[16,240]{1,0:T(8,128)S(1)} %concatenate.19.table_ref), custom_call_target="tpu_custom_call" | custom-call | tf_op jit(solution)/shard_map/triangle/pallas_call | solution.py:174
  58.2 9.6 %all-to-all-start.1 = ((bf16[128,36,128]{2,1,0:T(8,128)(2,1)}), bf16[128,36,128]{2,1,0:T(8,128)(2,1)S(1)}, u32[]{:S(2)}, u32[]{:S(2)}) async-start(bf16[128,36,128]{2,1,0:T(8,128)(2,1)} %triangle.1.refs_8_), calls=%async_computation.1 | async-start | bytes 2621440 | tf_op jit(solution)/shard_map/all_to_all | solution.py:34
  67.9 0.0 copy-start.19
  67.9 1.6 collective-permute-start.6
  69.4 2.9 %collective-permute-start.7 = (bf16[6,96,128]{2,1,0:T(8,128)(2,1)S(1)}, bf16[6,96,128]{2,1,0:T(8,128)(2,1)S(1)}, u32[]{:S(2)}, u32[]{:S(2)}) collective-permute-start(bf16[6,96,128]{2,1,0:T(8,128)(2,1)S(1)} %copy-done.28), channel_id=1, source_target_pairs={{0,2},{1,3},{2,4},{3,5},{4,6},{5,7},{6,0},{7,1},{8,10},{9,11},{10,... | collective-permute-start | bytes 442376 | tf_op jit(solution)/shard_map/ppermute | solution.py:569
  72.4 3.5 %collective-permute-start.8 = (bf16[6,96,128]{2,1,0:T(8,128)(2,1)S(1)}, bf16[6,96,128]{2,1,0:T(8,128)(2,1)S(1)}, u32[]{:S(2)}, u32[]{:S(2)}) collective-permute-start(bf16[6,96,128]{2,1,0:T(8,128)(2,1)S(1)} %copy-done.27), channel_id=1, source_target_pairs={{0,3},{1,4},{2,5},{3,6},{4,7},{5,0},{6,1},{7,2},{8,11},{9,12},{10,... | collective-permute-start | bytes 442376 | tf_op jit(solution)/shard_map/ppermute | solution.py:569
  75.8 0.1 collective-permute-start.9
  76.0 3.1 %collective-permute-start.10 = (bf16[6,96,128]{2,1,0:T(8,128)(2,1)S(1)}, bf16[6,96,128]{2,1,0:T(8,128)(2,1)S(1)}, u32[]{:S(2)}, u32[]{:S(2)}) collective-permute-start(bf16[6,96,128]{2,1,0:T(8,128)(2,1)S(1)} %copy-done.25), channel_id=1, source_target_pairs={{0,5},{1,6},{2,7},{3,0},{4,1},{5,2},{6,3},{7,4},{8,13},{9,14},{10,... | collective-permute-start | bytes 442376 | tf_op jit(solution)/shard_map/ppermute | solution.py:569
  79.1 12.6 %collective-permute-done.6.refs_1_ = bf16[6,96,128]{2,1,0:T(8,128)(2,1)S(1)} collective-permute-done((bf16[6,96,128]{2,1,0:T(8,128)(2,1)S(1)}, bf16[6,96,128]{2,1,0:T(8,128)(2,1)S(1)}, u32[]{:S(2)}, u32[]{:S(2)}) %collective-permute-start.6) | collective-permute-done | bytes 147488 | tf_op jit(solution)/shard_map/ppermute | solution.py:569
  91.7 1.9 collective-permute-start.11
  93.6 0.0 collective-permute-done.7.refs_2_
  93.6 1.5 collective-permute-start.12
  95.1 0.1 pad_add_fusion.place_ref
  95.2 0.0 collective-permute-done.8.refs_3_
  95.2 2.9 %collective-permute-done.10.refs_5_ = bf16[6,96,128]{2,1,0:T(8,128)(2,1)S(1)} collective-permute-done((bf16[6,96,128]{2,1,0:T(8,128)(2,1)S(1)}, bf16[6,96,128]{2,1,0:T(8,128)(2,1)S(1)}, u32[]{:S(2)}, u32[]{:S(2)}) %collective-permute-start.10) | collective-permute-done | bytes 147488 | tf_op jit(solution)/shard_map/ppermute | solution.py:569
  98.1 0.0 collective-permute-done.11.refs_6_
  98.1 5.0 %collective-permute-done.12.refs_7_ = bf16[6,96,128]{2,1,0:T(8,128)(2,1)S(1)} collective-permute-done((bf16[6,96,128]{2,1,0:T(8,128)(2,1)S(1)}, bf16[6,96,128]{2,1,0:T(8,128)(2,1)S(1)}, u32[]{:S(2)}, u32[]{:S(2)}) %collective-permute-start.12) | collective-permute-done | bytes 147488 | tf_op jit(solution)/shard_map/ppermute | solution.py:569
  103.1 0.6 copy-done.14
  103.8 0.0 copy-start.5
  103.8 0.0 copy-start.6
  103.8 2.5 %split.1 = (bf16[8,6,48,128]{3,2,1,0:T(8,128)(2,1)}, bf16[8,6,48,128]{3,2,1,0:T(8,128)(2,1)}) custom-call(s32[1]{0:T(128)} %bitcast.core_ref, bf16[6,96,128]{2,1,0:T(8,128)(2,1)} %get-tuple-element.24.refs_0_, bf16[6,96,128]{2,1,0:T(8,128)(2,1)} %copy-done.8, bf16[6,96,128]{2,1,0:T(8,128)(2,1)} %copy-done.9, bf16[6,96,128]{2,1,0:T(8,128)(2,1)} %copy-done.10, ...), custom_call_target="tpu_custom_call" | custom-call | tf_op jit(solution)/shard_map/split/pallas_call | solution.py:200
  106.3 0.6 collective-permute-start.13
  106.9 0.8 slice.12.wgo_ref
  107.6 0.1 copy.27.gain_sum_ref
  107.8 0.6 gather_fusion
  108.4 0.1 reshape.62
  108.5 0.1 reshape.65.far_ref
  108.6 0.1 reshape.63
  108.7 0.2 dynamic-slice_reduce_fusion
  108.9 0.1 reshape.64.near_ref
  108.9 0.0 copy-done.4
  109.0 0.0 copy-start.3
  109.0 1.1 copy-done.3
  110.0 7.1 %update.1 = (bf16[12,384,128]{2,1,0:T(8,128)(2,1)S(1)}, bf16[12,384,128]{2,1,0:T(8,128)(2,1)S(1)}, bf16[8,2,8,24,384]{4,3,2,1,0:T(8,128)(2,1)S(1)}) custom-call(s32[2]{0:T(128)S(1)} %pad_add_fusion.place_ref, bf16[128,36,128]{2,1,0:T(8,128)(2,1)S(1)} %all-to-all-done.1.back_ref, bf16[8,6,48,128]{3,2,1,0:T(8,128)(2,1)S(1)} %copy-done.3, ...), custom_call_target="tpu_custom_call" | custom-call | tf_op jit(solution)/shard_map/update/pallas_call | solution.py:326
  117.1 1.5 copy-done
  118.6 1.0 copy-done.1
  119.6 9.1 %all-to-all-start.2 = ((bf16[128,24,384]{2,1,0:T(8,128)(2,1)}), bf16[128,24,384]{2,1,0:T(8,128)(2,1)}, u32[]{:S(2)}, u32[]{:S(2)}) async-start(bf16[128,24,384]{2,1,0:T(8,128)(2,1)} %bitcast.31), calls=%async_computation.2 | async-start | bytes 4718592 | tf_op jit(solution)/shard_map/all_to_all | solution.py:34
  128.7 1.2 collective-permute-start.14
  129.9 0.6 fusion.2
  130.6 0.7 copy.32
  131.3 0.7 copy.31
  132.0 0.4 collective-permute-done.14.other_ref
  132.4 1.0 copy-done.7
  133.4 5.7 %project.1 = (bf16[12,384,128]{2,1,0:T(8,128)(2,1)}, bf16[12,768,128]{2,1,0:T(8,128)(2,1)}, bf16[12,4,48,768]{3,2,1,0:T(8,128)(2,1)}, f32[12,128,384]{2,1,0:T(8,128)}) custom-call(s32[1]{0:T(128)} %bitcast.core_ref, bf16[12,384,128]{2,1,0:T(8,128)(2,1)} %copy-done.2, bf16[12,384,128]{2,1,0:T(8,128)(2,1)} %copy-done.7, bf16[128,128]{1,0:T(8,128)(2,1)} %wq_ref.1, ...), custom_call_target="tpu_custom_call" | custom-call | tf_op jit(solution)/shard_map/project/pallas_call | solution.py:391
  139.1 21.9 %all-to-all-done.2.bias_ref = bf16[128,24,384]{2,1,0:T(8,128)(2,1)} async-done(((bf16[128,24,384]{2,1,0:T(8,128)(2,1)}), bf16[128,24,384]{2,1,0:T(8,128)(2,1)}, u32[]{:S(2)}, u32[]{:S(2)}) %all-to-all-start.2) | async-done | bytes 2359328 | tf_op jit(solution)/shard_map/all_to_all | solution.py:34
  161.0 31.0 %attention.1 = bf16[2,8,6,48,128]{4,3,2,1,0:T(8,128)(2,1)} custom-call(bf16[12,384,128]{2,1,0:T(8,128)(2,1)} %get-tuple-element.35.q_ref, bf16[12,768,128]{2,1,0:T(8,128)(2,1)} %get-tuple-element.36.k_ref, bf16[12,4,48,768]{3,2,1,0:T(8,128)(2,1)} %get-tuple-element.37.vt_ref, f32[12,128,384]{2,1,0:T(8,128)} %get-tuple-element.38.gate_ref, ...), custom_call_target="tpu_custom_call" | custom-call | tf_op jit(solution)/shard_map/attention/pallas_call | solution.py:512
  192.0 24.3 %all_to_all.20 = bf16[16,6,48,128]{3,2,1,0:T(8,128)(2,1)S(1)} all-to-all(bf16[16,6,48,128]{3,2,1,0:T(8,128)(2,1)} %bitcast.35), channel_id=1, replica_groups=mesh['rh'=8,'core'=2,'col'=8] {'core','col'}, dimensions={0} | all-to-all | bytes 2359296 | tf_op jit(solution)/shard_map/all_to_all | solution.py:34
  216.2 1.1 copy.30
  (66 shorter events, 0.2 us)
Async XLA Ops:
  8.4 11.5 %copy-start.21 = (s32[48]{0:T(128)S(1)}, s32[48]{0:T(128)}, u32[]{:S(2)}) copy-start(s32[48]{0:T(128)} %param.18) | copy-start | bytes 580
  8.4 11.6 %copy-start.22 = (s32[48]{0:T(128)S(1)}, s32[48]{0:T(128)}, u32[]{:S(2)}) copy-start(s32[48]{0:T(128)} %param.17) | copy-start | bytes 580
  8.4 11.6 %copy-start.17 = (f32[3,48]{1,0:T(4,128)S(1)}, f32[3,48]{1,0:T(4,128)}, u32[]{:S(2)}) copy-start(f32[3,48]{1,0:T(4,128)} %param.16) | copy-start | bytes 1732
  8.4 45.4 %all-to-all-start = ((bf16[128,72,128]{2,1,0:T(8,128)(2,1)}), bf16[128,72,128]{2,1,0:T(8,128)(2,1)S(1)}, u32[]{:S(2)}, u32[]{:S(2)}) async-start(bf16[128,72,128]{2,1,0:T(8,128)(2,1)} %get-tuple-element.23), calls=%async_computation | async-start | bytes 4718592 | tf_op jit(solution)/shard_map/all_to_all | solution.py:34
  20.1 24.5 %collective-permute-start.2 = (f32[1,240]{1,0:T(1,128)S(1)}, f32[1,240]{1,0:T(1,128)S(1)}, u32[]{:S(2)}, u32[]{:S(2)}) collective-permute-start(f32[1,240]{1,0:T(1,128)S(1)} %reshape.61), channel_id=1, source_target_pairs={{0,24},{8,16},{16,8},{24,0},{32,56},{40,48},{48,40},{56,32},{64,88... | collective-permute-start | bytes 2888 | tf_op jit(solution)/shard_map/ppermute | solution.py:579
  21.7 22.9 %collective-permute-start.1 = (f32[1,240]{1,0:T(1,128)S(1)}, f32[1,240]{1,0:T(1,128)S(1)}, u32[]{:S(2)}, u32[]{:S(2)}) collective-permute-start(f32[1,240]{1,0:T(1,128)S(1)} %reshape.61), channel_id=1, source_target_pairs={{0,16},{8,24},{16,0},{24,8},{32,48},{40,56},{48,32},{56,40},{64,80... | collective-permute-start | bytes 2888 | tf_op jit(solution)/shard_map/ppermute | solution.py:579
  22.5 22.1 %collective-permute-start = (f32[1,240]{1,0:T(1,128)S(1)}, f32[1,240]{1,0:T(1,128)S(1)}, u32[]{:S(2)}, u32[]{:S(2)}) collective-permute-start(f32[1,240]{1,0:T(1,128)S(1)} %reshape.61), channel_id=1, source_target_pairs={{0,8},{8,0},{16,24},{24,16},{32,40},{40,32},{48,56},{56,48},{64,72... | collective-permute-start | bytes 2888 | tf_op jit(solution)/shard_map/ppermute | solution.py:579
  44.6 6.1 %collective-permute-start.5 = (f32[4,240]{1,0:T(4,128)S(1)}, f32[4,240]{1,0:T(4,128)S(1)}, u32[]{:S(2)}, u32[]{:S(2)}) collective-permute-start(f32[4,240]{1,0:T(4,128)S(1)} %pad_maximum_fusion.2), channel_id=1, source_target_pairs={{0,96},{8,104},{16,112},{24,120},{32,64},{40,72},{48,80},{56,88},{... | collective-permute-start | bytes 11528 | tf_op jit(solution)/shard_map/ppermute | solution.py:579
  49.5 4.3 %collective-permute-start.4 = (f32[4,240]{1,0:T(4,128)S(1)}, f32[4,240]{1,0:T(4,128)S(1)}, u32[]{:S(2)}, u32[]{:S(2)}) collective-permute-start(f32[4,240]{1,0:T(4,128)S(1)} %pad_maximum_fusion.2), channel_id=1, source_target_pairs={{0,64},{8,72},{16,80},{24,88},{32,96},{40,104},{48,112},{56,120},{... | collective-permute-start | bytes 11528 | tf_op jit(solution)/shard_map/ppermute | solution.py:579
  49.9 3.9 %collective-permute-start.3 = (f32[4,240]{1,0:T(4,128)S(1)}, f32[4,240]{1,0:T(4,128)S(1)}, u32[]{:S(2)}, u32[]{:S(2)}) collective-permute-start(f32[4,240]{1,0:T(4,128)S(1)} %pad_maximum_fusion.2), channel_id=1, source_target_pairs={{0,32},{8,40},{16,48},{24,56},{32,0},{40,8},{48,16},{56,24},{64,96... | collective-permute-start | bytes 11528 | tf_op jit(solution)/shard_map/ppermute | solution.py:579
  58.2 9.7 %copy-start.29 = (bf16[6,96,128]{2,1,0:T(8,128)(2,1)S(1)}, bf16[6,96,128]{2,1,0:T(8,128)(2,1)}, u32[]{:S(2)}) copy-start(bf16[6,96,128]{2,1,0:T(8,128)(2,1)} %get-tuple-element.25) | copy-start | bytes 442372
  58.2 11.2 %copy-start.28 = (bf16[6,96,128]{2,1,0:T(8,128)(2,1)S(1)}, bf16[6,96,128]{2,1,0:T(8,128)(2,1)}, u32[]{:S(2)}) copy-start(bf16[6,96,128]{2,1,0:T(8,128)(2,1)} %get-tuple-element.26) | copy-start | bytes 442372
  58.2 14.2 %copy-start.27 = (bf16[6,96,128]{2,1,0:T(8,128)(2,1)S(1)}, bf16[6,96,128]{2,1,0:T(8,128)(2,1)}, u32[]{:S(2)}) copy-start(bf16[6,96,128]{2,1,0:T(8,128)(2,1)} %get-tuple-element.27) | copy-start | bytes 442372
  58.2 17.6 %copy-start.26 = (bf16[6,96,128]{2,1,0:T(8,128)(2,1)S(1)}, bf16[6,96,128]{2,1,0:T(8,128)(2,1)}, u32[]{:S(2)}) copy-start(bf16[6,96,128]{2,1,0:T(8,128)(2,1)} %get-tuple-element.28) | copy-start | bytes 442372
  58.2 17.8 %copy-start.25 = (bf16[6,96,128]{2,1,0:T(8,128)(2,1)S(1)}, bf16[6,96,128]{2,1,0:T(8,128)(2,1)}, u32[]{:S(2)}) copy-start(bf16[6,96,128]{2,1,0:T(8,128)(2,1)} %get-tuple-element.29) | copy-start | bytes 442372
  58.2 33.5 %copy-start.24 = (bf16[6,96,128]{2,1,0:T(8,128)(2,1)S(1)}, bf16[6,96,128]{2,1,0:T(8,128)(2,1)}, u32[]{:S(2)}) copy-start(bf16[6,96,128]{2,1,0:T(8,128)(2,1)} %get-tuple-element.30) | copy-start | bytes 442372
  58.2 35.4 %copy-start.23 = (bf16[6,96,128]{2,1,0:T(8,128)(2,1)S(1)}, bf16[6,96,128]{2,1,0:T(8,128)(2,1)}, u32[]{:S(2)}) copy-start(bf16[6,96,128]{2,1,0:T(8,128)(2,1)} %get-tuple-element.31) | copy-start | bytes 442372
  58.2 50.7 %all-to-all-start.1 = ((bf16[128,36,128]{2,1,0:T(8,128)(2,1)}), bf16[128,36,128]{2,1,0:T(8,128)(2,1)S(1)}, u32[]{:S(2)}, u32[]{:S(2)}) async-start(bf16[128,36,128]{2,1,0:T(8,128)(2,1)} %triangle.1.refs_8_), calls=%async_computation.1 | async-start | bytes 2621440 | tf_op jit(solution)/shard_map/all_to_all | solution.py:34
  67.9 39.8 %copy-start.19 = (f32[128]{0:T(128)S(1)}, f32[128]{0:T(128)}, u32[]{:S(2)}) copy-start(f32[128]{0:T(128)} %param.20) | copy-start | bytes 1540
  67.9 23.8 %collective-permute-start.6 = (bf16[6,96,128]{2,1,0:T(8,128)(2,1)S(1)}, bf16[6,96,128]{2,1,0:T(8,128)(2,1)S(1)}, u32[]{:S(2)}, u32[]{:S(2)}) collective-permute-start(bf16[6,96,128]{2,1,0:T(8,128)(2,1)S(1)} %copy-done.29), channel_id=1, source_target_pairs={{0,1},{1,2},{2,3},{3,4},{4,5},{5,6},{6,7},{7,0},{8,9},{9,10},{10,1... | collective-permute-start | bytes 442376 | tf_op jit(solution)/shard_map/ppermute | solution.py:569
  69.4 24.2 %collective-permute-start.7 = (bf16[6,96,128]{2,1,0:T(8,128)(2,1)S(1)}, bf16[6,96,128]{2,1,0:T(8,128)(2,1)S(1)}, u32[]{:S(2)}, u32[]{:S(2)}) collective-permute-start(bf16[6,96,128]{2,1,0:T(8,128)(2,1)S(1)} %copy-done.28), channel_id=1, source_target_pairs={{0,2},{1,3},{2,4},{3,5},{4,6},{5,7},{6,0},{7,1},{8,10},{9,11},{10,... | collective-permute-start | bytes 442376 | tf_op jit(solution)/shard_map/ppermute | solution.py:569
  72.4 22.8 %collective-permute-start.8 = (bf16[6,96,128]{2,1,0:T(8,128)(2,1)S(1)}, bf16[6,96,128]{2,1,0:T(8,128)(2,1)S(1)}, u32[]{:S(2)}, u32[]{:S(2)}) collective-permute-start(bf16[6,96,128]{2,1,0:T(8,128)(2,1)S(1)} %copy-done.27), channel_id=1, source_target_pairs={{0,3},{1,4},{2,5},{3,6},{4,7},{5,0},{6,1},{7,2},{8,11},{9,12},{10,... | collective-permute-start | bytes 442376 | tf_op jit(solution)/shard_map/ppermute | solution.py:569
  75.8 19.4 %collective-permute-start.9 = (bf16[6,96,128]{2,1,0:T(8,128)(2,1)S(1)}, bf16[6,96,128]{2,1,0:T(8,128)(2,1)S(1)}, u32[]{:S(2)}, u32[]{:S(2)}) collective-permute-start(bf16[6,96,128]{2,1,0:T(8,128)(2,1)S(1)} %copy-done.26), channel_id=1, source_target_pairs={{0,4},{1,5},{2,6},{3,7},{4,0},{5,1},{6,2},{7,3},{8,12},{9,13},{10,... | collective-permute-start | bytes 442376 | tf_op jit(solution)/shard_map/ppermute | solution.py:569
  76.0 22.1 %collective-permute-start.10 = (bf16[6,96,128]{2,1,0:T(8,128)(2,1)S(1)}, bf16[6,96,128]{2,1,0:T(8,128)(2,1)S(1)}, u32[]{:S(2)}, u32[]{:S(2)}) collective-permute-start(bf16[6,96,128]{2,1,0:T(8,128)(2,1)S(1)} %copy-done.25), channel_id=1, source_target_pairs={{0,5},{1,6},{2,7},{3,0},{4,1},{5,2},{6,3},{7,4},{8,13},{9,14},{10,... | collective-permute-start | bytes 442376 | tf_op jit(solution)/shard_map/ppermute | solution.py:569
  91.7 11.4 %copy-start.8 = (bf16[6,96,128]{2,1,0:T(8,128)(2,1)}, bf16[6,96,128]{2,1,0:T(8,128)(2,1)S(1)}, u32[]{:S(2)}) copy-start(bf16[6,96,128]{2,1,0:T(8,128)(2,1)S(1)} %collective-permute-done.6.refs_1_) | copy-start | bytes 442372
  91.7 6.4 %collective-permute-start.11 = (bf16[6,96,128]{2,1,0:T(8,128)(2,1)S(1)}, bf16[6,96,128]{2,1,0:T(8,128)(2,1)S(1)}, u32[]{:S(2)}, u32[]{:S(2)}) collective-permute-start(bf16[6,96,128]{2,1,0:T(8,128)(2,1)S(1)} %copy-done.24), channel_id=1, source_target_pairs={{0,6},{1,7},{2,0},{3,1},{4,2},{5,3},{6,4},{7,5},{8,14},{9,15},{10,... | collective-permute-start | bytes 442376 | tf_op jit(solution)/shard_map/ppermute | solution.py:569
  93.6 9.5 %copy-start.9 = (bf16[6,96,128]{2,1,0:T(8,128)(2,1)}, bf16[6,96,128]{2,1,0:T(8,128)(2,1)S(1)}, u32[]{:S(2)}) copy-start(bf16[6,96,128]{2,1,0:T(8,128)(2,1)S(1)} %collective-permute-done.7.refs_2_) | copy-start | bytes 442372
  93.6 9.5 %collective-permute-start.12 = (bf16[6,96,128]{2,1,0:T(8,128)(2,1)S(1)}, bf16[6,96,128]{2,1,0:T(8,128)(2,1)S(1)}, u32[]{:S(2)}, u32[]{:S(2)}) collective-permute-start(bf16[6,96,128]{2,1,0:T(8,128)(2,1)S(1)} %copy-done.23), channel_id=1, source_target_pairs={{0,7},{1,0},{2,1},{3,2},{4,3},{5,4},{6,5},{7,6},{8,15},{9,8},{10,9... | collective-permute-start | bytes 442376 | tf_op jit(solution)/shard_map/ppermute | solution.py:569
  95.2 7.9 %copy-start.10 = (bf16[6,96,128]{2,1,0:T(8,128)(2,1)}, bf16[6,96,128]{2,1,0:T(8,128)(2,1)S(1)}, u32[]{:S(2)}) copy-start(bf16[6,96,128]{2,1,0:T(8,128)(2,1)S(1)} %collective-permute-done.8.refs_3_) | copy-start | bytes 442372
  95.2 7.9 %copy-start.11 = (bf16[6,96,128]{2,1,0:T(8,128)(2,1)}, bf16[6,96,128]{2,1,0:T(8,128)(2,1)S(1)}, u32[]{:S(2)}) copy-start(bf16[6,96,128]{2,1,0:T(8,128)(2,1)S(1)} %collective-permute-done.9.refs_4_) | copy-start | bytes 442372
  98.1 5.0 %copy-start.12 = (bf16[6,96,128]{2,1,0:T(8,128)(2,1)}, bf16[6,96,128]{2,1,0:T(8,128)(2,1)S(1)}, u32[]{:S(2)}) copy-start(bf16[6,96,128]{2,1,0:T(8,128)(2,1)S(1)} %collective-permute-done.10.refs_5_) | copy-start | bytes 442372
  98.1 5.0 %copy-start.13 = (bf16[6,96,128]{2,1,0:T(8,128)(2,1)}, bf16[6,96,128]{2,1,0:T(8,128)(2,1)S(1)}, u32[]{:S(2)}) copy-start(bf16[6,96,128]{2,1,0:T(8,128)(2,1)S(1)} %collective-permute-done.11.refs_6_) | copy-start | bytes 442372
  103.1 0.7 copy-start.14
  103.7 4.0 %copy-start.18 = (bf16[128,4]{0,1:T(4,128)(2,1)S(1)}, bf16[128,4]{0,1:T(4,128)(2,1)}, u32[]{:S(2)}) copy-start(bf16[128,4]{0,1:T(4,128)(2,1)} %param.28) | copy-start | bytes 3076
  103.7 4.0 %copy-start.16 = (f32[36,128]{1,0:T(8,128)S(1)}, f32[36,128]{1,0:T(8,128)}, u32[]{:S(2)}) copy-start(f32[36,128]{1,0:T(8,128)} %param.24) | copy-start | bytes 55300
  103.7 4.0 %copy-start.20 = (f32[128]{0:T(128)S(1)}, f32[128]{0:T(128)}, u32[]{:S(2)}) copy-start(f32[128]{0:T(128)} %param.25) | copy-start | bytes 1540
  103.7 5.2 %copy-start.4 = (bf16[128,128]{1,0:T(8,128)(2,1)S(1)}, bf16[128,128]{1,0:T(8,128)(2,1)}, u32[]{:S(2)}) copy-start(bf16[128,128]{1,0:T(8,128)(2,1)} %wout_ref.1) | copy-start | bytes 98308
  103.8 5.2 %copy-start.5 = (f32[128]{0:T(128)S(1)}, f32[128]{0:T(128)}, u32[]{:S(2)}) copy-start(f32[128]{0:T(128)} %param.19) | copy-start | bytes 1540
  103.8 5.2 %copy-start.6 = (f32[128]{0:T(128)S(1)}, f32[128]{0:T(128)}, u32[]{:S(2)}) copy-start(f32[128]{0:T(128)} %param.21) | copy-start | bytes 1540
  106.3 2.7 %collective-permute-start.13 = (bf16[8,6,48,128]{3,2,1,0:T(8,128)(2,1)}, bf16[8,6,48,128]{3,2,1,0:T(8,128)(2,1)S(1)}, u32[]{:S(2)}, u32[]{:S(2)}) collective-permute-start(bf16[8,6,48,128]{3,2,1,0:T(8,128)(2,1)} %get-tuple-element.33), channel_id=1, source_target_pairs={{0,8},{8,0},{1,9},{9,1},{2,10},{10,2},{3,11},{11,3},{4,12},{12,4},... | collective-permute-start | bytes 1769480 | tf_op jit(solution)/shard_map/ppermute | solution.py:591
  109.0 1.1 copy-start.3
  117.1 1.5 copy-start
  118.6 1.0 copy-start.1
  119.6 9.1 %copy-start.2 = (bf16[12,384,128]{2,1,0:T(8,128)(2,1)}, bf16[12,384,128]{2,1,0:T(8,128)(2,1)S(1)}, u32[]{:S(2)}) copy-start(bf16[12,384,128]{2,1,0:T(8,128)(2,1)S(1)} %get-tuple-element.34.own_ref) | copy-start | bytes 3538948
  119.6 10.3 %copy-start.15 = (bf16[128,384]{1,0:T(8,128)(2,1)S(1)}, bf16[128,384]{1,0:T(8,128)(2,1)}, u32[]{:S(2)}) copy-start(bf16[128,384]{1,0:T(8,128)(2,1)} %param.27) | copy-start | bytes 294916
  119.6 41.4 %all-to-all-start.2 = ((bf16[128,24,384]{2,1,0:T(8,128)(2,1)}), bf16[128,24,384]{2,1,0:T(8,128)(2,1)}, u32[]{:S(2)}, u32[]{:S(2)}) async-start(bf16[128,24,384]{2,1,0:T(8,128)(2,1)} %bitcast.31), calls=%async_computation.2 | async-start | bytes 4718592 | tf_op jit(solution)/shard_map/all_to_all | solution.py:34
  128.7 3.7 %collective-permute-start.14 = (bf16[12,384,128]{2,1,0:T(8,128)(2,1)S(1)}, bf16[12,384,128]{2,1,0:T(8,128)(2,1)S(1)}, u32[]{:S(2)}, u32[]{:S(2)}) collective-permute-start(bf16[12,384,128]{2,1,0:T(8,128)(2,1)S(1)} %get-tuple-element.34.own_ref), channel_id=1, source_target_pairs={{0,8},{1,9},{2,10},{3,11},{4,12},{5,13},{6,14},{7,15},{8,0},{9,1},... | collective-permute-start | bytes 3538952 | tf_op jit(solution)/shard_map/ppermute | solution.py:611
  132.4 1.0 copy-start.7
